TPU v7x, 32 devices: a whole 2x2x4 slice. The times are simulated.
32 devices in a mesh: parts: 2 (over y), mesh: 4 (over z), tile: 2 (over x), feat: 2 (over core).
Axes of the slice: x: 2, y: 2, z: 4, core: 2. Of those that a mesh axis runs over, the one named last changes fastest.
Arguments:
- fields: bfloat16 [2048, 128], P(('parts', 'mesh', 'tile')), parts along dimension 0, may hold values from -6 to 6
- owner_group: int32 [1024, 1], P(('mesh', 'tile')), may hold values from 0 to 7; in each aligned block of 128 rows (0 to 127, 128 to 255, ...) at most 32 rows name the same one
- owner_node: int32 [1024], P(('mesh', 'tile')), may hold values from 0 to 31
- stencil_codes: int32 [256, 8], P(('mesh', 'tile')), may hold values from 0 to 24
- coarse_ids: int32 [256], P(('mesh', 'tile')), may hold values from 0 to 15
- encode_weight: bfloat16 [128, 512], P(None, 'feat'), may hold values from -0.5 to 0.5
- process_weight: bfloat16 [512, 512], P(None, 'feat'), may hold values from -0.09375 to 0.09375
- coarse_weight: bfloat16 [512, 512], P(None, 'feat'), may hold values from -0.0625 to 0.0625
- decode_weight: bfloat16 [512, 128], P('feat'), may hold values from -0.25 to 0.25
- cotangent: float32 [2048, 128], P(('parts', 'mesh', 'tile')), parts along dimension 0, may hold values from -6 to 6
Outputs:
- prediction: float32 [2048, 128], P(('parts', 'mesh', 'tile')), parts along dimension 0
- encode_grad: float32 [256, 512], P('parts', 'feat'), parts along dimension 0
- process_grad: float32 [1024, 512], P('parts', 'feat'), parts along dimension 0
- coarse_grad: float32 [1024, 512], P('parts', 'feat'), parts along dimension 0
- decode_grad: float32 [1024, 128], P(('parts', 'feat')), parts along dimension 0
There are 2 independent parts, one for each index of `parts`. A program takes and returns all parts, laid end to end along the dimension named above; an argument that names none is the same for every part. Nothing has to cross between parts.
Inputs may be any that keep to these rules, and one draw needn't show every extreme that they name: `owner_group`: in the rows of one device group no value is named more than 32 times.
All inputs are finite; a program needn't handle non-finite values.
Results may differ from a plain program's by a relative error of at most 0.0073.
Values may be sent and summed in bfloat16 or wider, within the bound.
No kernel may reach another device: no remote copies, remote signals or barrier semaphores. Data moves between devices by JAX's collectives and lax.ppermute only.
A program may use at most 64 MiB of HBM per device.

v0:
```python
import jax
import jax.numpy as jnp
from jax import lax
from jax.sharding import PartitionSpec as P

MA = 4
MB = 8
CPD = 2


def padded(array, sides, width):
    for axis, dim in sides:
        peers, length = (lax.axis_size(axis), array.shape[dim])
        up = [(i, (i + 1) % peers) for i in range(peers)]
        down = [(j, i) for i, j in up]
        last = lax.slice_in_dim(array, length - width, length, axis=dim)
        initial = lax.slice_in_dim(array, 0, width, axis=dim)
        before = lax.ppermute(last, axis, up)
        after = lax.ppermute(initial, axis, down)
        array = jnp.concatenate([before, array, after], axis=dim)
    return array


def silu_grad(pre):
    sig = jax.nn.sigmoid(pre)
    return sig * (1.0 + pre * (1.0 - sig))


def send_rows(outgoing, slot_node):
    feat_width = outgoing.shape[-1]
    got, got_node = (
        lax.all_to_all(outgoing, ("mesh", "tile"), split_axis=0, concat_axis=0, tiled=True),
        lax.all_to_all(slot_node, ("mesh", "tile"), split_axis=0, concat_axis=0, tiled=True),
    )
    return (got.reshape(-1, feat_width), got_node.reshape(-1))


def route_block(block, mesh_count, tile_count, purpose):
    feat_width = block.shape[-1]
    slot_count = block.shape[0] // (mesh_count * tile_count)
    flat_shape = (mesh_count * tile_count, slot_count, feat_width)
    if purpose == "reply":
        moved = lax.all_to_all(
            block.reshape(flat_shape), ("mesh", "tile"), split_axis=0, concat_axis=0, tiled=True
        )
    elif purpose == "gradient":
        moved = lax.all_to_all(
            block.reshape(flat_shape), ("mesh", "tile"), split_axis=0, concat_axis=0, tiled=True
        )
    else:
        moved = lax.all_to_all(
            block.reshape(flat_shape), ("mesh", "tile"), split_axis=0, concat_axis=0, tiled=True
        )
    return moved.reshape(-1, feat_width)


def body(
    fields,
    owner_group,
    owner_node,
    stencil_codes,
    coarse_ids,
    encode_weight,
    process_weight,
    coarse_weight,
    decode_weight,
    cotangent,
):
    highest = lax.Precision.HIGHEST
    row_count = fields.shape[0]
    mesh_count = lax.axis_size("mesh")
    tile_count = lax.axis_size("tile")
    groups = mesh_count * tile_count
    slot_count = 2 * row_count // groups
    feat_width = encode_weight.shape[1]
    patch_rows = MA
    patch_cols = MB
    nodes_local = patch_rows * patch_cols
    coarse_count = CPD * groups
    target = owner_group[:, 0]
    group_onehot = (target[:, None] == jnp.arange(groups, dtype=jnp.int32)[None, :]).astype(
        jnp.int32
    )
    earlier = jnp.cumsum(group_onehot, axis=0) - group_onehot
    position = target * slot_count + jnp.sum(earlier * group_onehot, axis=1)
    matches = jnp.arange(groups * slot_count, dtype=jnp.int32)[:, None] == position[None, :]
    dispatch = matches.astype(jnp.bfloat16)
    slot_node = (jnp.max(jnp.where(matches, owner_node[None, :] + 1, 0), axis=1) - 1).reshape(
        groups, slot_count
    )
    pre_encode = jnp.dot(fields, encode_weight, preferred_element_type=jnp.float32)
    hidden = jax.nn.silu(pre_encode).astype(jnp.bfloat16)
    outgoing = jnp.dot(dispatch, hidden, preferred_element_type=jnp.float32).astype(jnp.bfloat16)
    incoming, incoming_node = send_rows(outgoing.reshape(groups, slot_count, feat_width), slot_node)
    node_match = (
        incoming_node[:, None] == jnp.arange(nodes_local, dtype=jnp.int32)[None, :]
    ).astype(jnp.bfloat16)
    node_in = jnp.einsum(
        "sn,sh->nh", node_match, incoming, preferred_element_type=jnp.float32
    ).astype(jnp.bfloat16)
    counts = jnp.sum(
        (stencil_codes[:, :, None] == jnp.arange(25, dtype=jnp.int32)[None, None, :]).astype(
            jnp.float32
        ),
        axis=1,
    )
    counts = counts.astype(jnp.bfloat16).reshape(patch_rows, patch_cols, 25)
    padded_nodes, padded_counts = (
        padded(node_in.reshape(patch_rows, patch_cols, feat_width), (("mesh", 0), ("tile", 1)), 2),
        padded(counts, (("mesh", 0), ("tile", 1)), 2),
    )
    gathered = jnp.zeros((patch_rows, patch_cols, feat_width), jnp.float32)
    for code_index in range(25):
        step_x = code_index // 5 - 2
        step_y = code_index % 5 - 2
        weight_here = padded_counts[
            2 : 2 + patch_rows, 2 : 2 + patch_cols, code_index : code_index + 1
        ].astype(jnp.float32)
        gathered = gathered + weight_here * padded_nodes[
            2 + step_x : 2 + step_x + patch_rows, 2 + step_y : 2 + step_y + patch_cols
        ].astype(jnp.float32)
    agg = gathered.reshape(nodes_local, feat_width).astype(jnp.bfloat16)
    agg_full = lax.all_gather(agg, "feat", axis=1, tiled=True)
    pre_mesh = jnp.dot(agg_full, process_weight, preferred_element_type=jnp.float32)
    level_one = node_in.astype(jnp.float32) + jax.nn.silu(pre_mesh)
    coarse_match = (
        coarse_ids[:, None] == jnp.arange(coarse_count, dtype=jnp.int32)[None, :]
    ).astype(jnp.float32)
    coarse_part = jnp.dot(coarse_match.T, level_one, precision=highest)
    coarse_total = lax.psum(coarse_part, ("mesh", "tile"))
    coarse_in = lax.all_gather(coarse_total.astype(jnp.bfloat16), "feat", axis=1, tiled=True)
    pre_coarse = jnp.dot(coarse_in, coarse_weight, preferred_element_type=jnp.float32)
    coarse_out = jax.nn.silu(pre_coarse).astype(jnp.bfloat16)
    level_two = (
        level_one
        + jnp.dot(coarse_match.astype(jnp.bfloat16), coarse_out, preferred_element_type=jnp.float32)
    ).astype(jnp.bfloat16)
    reply_rows = jnp.dot(node_match, level_two, preferred_element_type=jnp.float32).astype(
        jnp.bfloat16
    )
    returned = route_block(reply_rows, mesh_count, tile_count, "reply")
    merged = (
        hidden.astype(jnp.float32)
        + jnp.einsum("sr,sh->rh", dispatch, returned, preferred_element_type=jnp.float32)
    ).astype(jnp.bfloat16)
    pred_part = jnp.dot(merged, decode_weight, preferred_element_type=jnp.float32)
    prediction = lax.psum(pred_part, "feat")
    decode_grad = jnp.dot(merged.astype(jnp.float32).T, cotangent, precision=highest)
    grad_merged = jnp.dot(cotangent, decode_weight.astype(jnp.float32).T, precision=highest)
    grad_out = jnp.dot(
        dispatch, grad_merged.astype(jnp.bfloat16), preferred_element_type=jnp.float32
    ).astype(jnp.bfloat16)
    grad_in = route_block(grad_out, mesh_count, tile_count, "gradient")
    grad_two = jnp.einsum("sn,sh->nh", node_match, grad_in, preferred_element_type=jnp.float32)
    coarse_grad_part = jnp.dot(coarse_match.T, grad_two, precision=highest)
    grad_coarse_out = lax.psum(coarse_grad_part, ("mesh", "tile"))
    grad_pre_coarse = grad_coarse_out * silu_grad(pre_coarse)
    coarse_grad = jnp.dot(coarse_in.astype(jnp.float32).T, grad_pre_coarse, precision=highest)
    grad_coarse_full = jnp.dot(
        grad_pre_coarse, coarse_weight.astype(jnp.float32).T, precision=highest
    )
    grad_coarse_in = lax.psum_scatter(grad_coarse_full, "feat", scatter_dimension=1, tiled=True)
    grad_one = grad_two + jnp.dot(coarse_match, grad_coarse_in, precision=highest)
    grad_pre_mesh = grad_one * silu_grad(pre_mesh)
    process_grad = jnp.dot(agg_full.astype(jnp.float32).T, grad_pre_mesh, precision=highest)
    grad_pre_full = lax.all_gather(grad_pre_mesh, "feat", axis=1, tiled=True)
    weight_full = lax.all_gather(process_weight, "feat", axis=1, tiled=True)
    own_rows = lax.dynamic_slice_in_dim(
        weight_full, lax.axis_index("feat") * feat_width, feat_width, 0
    )
    grad_agg = jnp.dot(grad_pre_full, own_rows.astype(jnp.float32).T, precision=highest).astype(
        jnp.bfloat16
    )
    padded_grad = padded(
        grad_agg.reshape(patch_rows, patch_cols, feat_width), (("mesh", 0), ("tile", 1)), 2
    )
    spread = jnp.zeros((patch_rows, patch_cols, feat_width), jnp.float32)
    for code_index in range(25):
        step_x = code_index // 5 - 2
        step_y = code_index % 5 - 2
        weight_there = padded_counts[
            2 - step_x : 2 - step_x + patch_rows,
            2 - step_y : 2 - step_y + patch_cols,
            code_index : code_index + 1,
        ].astype(jnp.float32)
        spread = spread + weight_there * padded_grad[
            2 - step_x : 2 - step_x + patch_rows, 2 - step_y : 2 - step_y + patch_cols
        ].astype(jnp.float32)
    grad_zero = (grad_one + spread.reshape(nodes_local, feat_width)).astype(jnp.bfloat16)
    back_rows = jnp.dot(node_match, grad_zero, preferred_element_type=jnp.float32).astype(
        jnp.bfloat16
    )
    grad_back = route_block(back_rows, mesh_count, tile_count, "return")
    grad_hidden = grad_merged + jnp.einsum(
        "sr,sh->rh", dispatch, grad_back, preferred_element_type=jnp.float32
    )
    grad_pre_encode = grad_hidden * silu_grad(pre_encode)
    encode_grad = jnp.dot(fields.astype(jnp.float32).T, grad_pre_encode, precision=highest)
    encode_grad, process_grad, decode_grad = lax.psum(
        (encode_grad, process_grad, decode_grad), ("mesh", "tile")
    )
    return (prediction, encode_grad, process_grad, coarse_grad, decode_grad)


def solution(mesh):
    placed = (
        P(("parts", "mesh", "tile"), None),
        P(("mesh", "tile"), None),
        P(("mesh", "tile")),
        P(("mesh", "tile"), None),
        P(("mesh", "tile")),
        P(None, "feat"),
        P(None, "feat"),
        P(None, "feat"),
        P("feat", None),
        P(("parts", "mesh", "tile"), None),
    )
    return jax.shard_map(
        body,
        mesh=mesh,
        in_specs=placed,
        out_specs=(
            P(("parts", "mesh", "tile"), None),
            P("parts", "feat"),
            P("parts", "feat"),
            P("parts", "feat"),
            P(("parts", "feat"), None),
        ),
        check_vma=False,
    )
```

profile of v0, /device:TPU:0, one launch (start us, length us, event | category | flops | bytes accessed | tf_op | source)
XLA Modules:
  0.0 239.0 jit_solution(17337681555565160139)
XLA Ops:
  9.6 7.3 %all-to-all-start = ((s32[8,1,32]{2,1,0:T(1,128)}), s32[8,1,32]{2,1,0:T(1,128)S(1)}, u32[]{:S(2)}, u32[]{:S(2)}) async-start(s32[8,1,32]{2,1,0:T(1,128)} %sub.20), calls=%async_computation | async-start | bytes 8192 | tf_op jit(solution)/shard_map/all_to_all | solution.py:33
  17.1 3.8 %collective-permute-start.5 = (bf16[2,8,25]{2,1,0:T(8,128)(2,1)S(1)}, bf16[2,8,25]{2,1,0:T(8,128)(2,1)S(1)}, u32[]{:S(2)}, u32[]{:S(2)}) collective-permute-start(bf16[2,8,25]{2,1,0:T(8,128)(2,1)S(1)} %bitcast.73), channel_id=1, source_target_pairs={{4,0},{8,4},{12,8},{0,12},{5,1},{9,5},{13,9},{1,13},{6,2},{10,6},{... | collective-permute-start | bytes 2408 | tf_op jit(solution)/shard_map/ppermute | solution.py:19
  23.2 2.2 all_gather.15
  26.5 1.5 collective-permute-start.6
  28.8 5.2 %all-to-all-start.1 = ((bf16[8,32,256]{2,1,0:T(8,128)(2,1)}), bf16[8,32,256]{2,1,0:T(8,128)(2,1)S(1)}, u32[]{:S(2)}, u32[]{:S(2)}) async-start(bf16[8,32,256]{2,1,0:T(8,128)(2,1)} %bitcast.1), calls=%async_computation.1 | async-start | bytes 262144 | tf_op jit(solution)/shard_map/all_to_all | solution.py:32
  35.6 5.8 %all-to-all-done.1 = bf16[8,32,256]{2,1,0:T(8,128)(2,1)S(1)} async-done(((bf16[8,32,256]{2,1,0:T(8,128)(2,1)}), bf16[8,32,256]{2,1,0:T(8,128)(2,1)S(1)}, u32[]{:S(2)}, u32[]{:S(2)}) %all-to-all-start.1) | async-done | bytes 131104 | tf_op jit(solution)/shard_map/all_to_all | solution.py:32
  41.4 3.4 %all-to-all-start.3 = ((bf16[8,32,256]{2,1,0:T(8,128)(2,1)}), bf16[8,32,256]{2,1,0:T(8,128)(2,1)S(1)}, u32[]{:S(2)}, u32[]{:S(2)}) async-start(bf16[8,32,256]{2,1,0:T(8,128)(2,1)} %bitcast.10), calls=%async_computation.3 | async-start | bytes 262144 | tf_op jit(solution)/shard_map/all_to_all | solution.py:47
  45.1 3.8 %collective-permute-start.1 = (bf16[2,8,256]{2,1,0:T(8,128)(2,1)S(1)}, bf16[2,8,256]{2,1,0:T(8,128)(2,1)S(1)}, u32[]{:S(2)}, u32[]{:S(2)}) collective-permute-start(bf16[2,8,256]{2,1,0:T(8,128)(2,1)S(1)} %get-tuple-element.96), channel_id=1, source_target_pairs={{4,0},{8,4},{12,8},{0,12},{5,1},{9,5},{13,9},{1,13},{6,2},{10,6},{... | collective-permute-start | bytes 24584 | tf_op jit(solution)/shard_map/ppermute | solution.py:19
  48.8 3.3 %all-to-all-done.3 = bf16[8,32,256]{2,1,0:T(8,128)(2,1)S(1)} async-done(((bf16[8,32,256]{2,1,0:T(8,128)(2,1)}), bf16[8,32,256]{2,1,0:T(8,128)(2,1)S(1)}, u32[]{:S(2)}, u32[]{:S(2)}) %all-to-all-start.3) | async-done | bytes 131104 | tf_op jit(solution)/shard_map/all_to_all | solution.py:47
  52.4 1.9 collective-permute-done
  54.3 1.5 collective-permute-start.2
  56.7 1.4 collective-permute-done.2
  58.0 1.5 collective-permute-done.3
  59.7 1.8 all_gather.12
  62.0 33.4 %all-reduce = (bf16[16,256]{1,0:T(8,128)(2,1)S(1)}, f32[16,256]{1,0:T(8,128)S(1)}) all-reduce(f32[16,256]{1,0:T(8,128)S(1)} %fusion.21, f32[16,256]{1,0:T(8,128)S(1)} %fusion.20), channel_id=1, replica_groups=mesh['parts'=2,'mesh'=4,'tile'=2,'feat'=2] {'mesh','tile'}, use_global_device_ids=true, to_apply=%region_4.5 | all-reduce | flops 8192 | bytes 57344 | tf_op jit(solution)/shard_map/psum | solution.py:130
  95.4 1.8 all_gather.13
  98.5 4.7 %reduce-scatter.2.cloned.1.call-done = f32[16,256]{1,0:T(8,128)} async-done(((f32[16,512]{1,0:T(8,128)}), f32[16,256]{1,0:T(8,128)}) %reduce-scatter.2.cloned.1.call-update) | async-done | bytes 16400 | tf_op jit(solution)/shard_map/reduce_scatter | solution.py:162
  104.2 1.9 all_gather.14
  106.4 1.8 collective-permute-start.7
  108.2 2.1 collective-permute-start.8
  111.3 3.9 %all-to-all-start.2 = ((bf16[8,32,256]{2,1,0:T(8,128)(2,1)}), bf16[8,32,256]{2,1,0:T(8,128)(2,1)S(1)}, u32[]{:S(2)}, u32[]{:S(2)}) async-start(bf16[8,32,256]{2,1,0:T(8,128)(2,1)} %bitcast.8), calls=%async_computation.2 | async-start | bytes 262144 | tf_op jit(solution)/shard_map/all_to_all | solution.py:43
  115.3 2.1 collective-permute-start.9
  117.4 1.2 fusion.45
  119.3 2.0 collective-permute-done.11
  122.6 4.1 %all-to-all-start.4 = ((bf16[8,32,256]{2,1,0:T(8,128)(2,1)}), bf16[8,32,256]{2,1,0:T(8,128)(2,1)S(1)}, u32[]{:S(2)}, u32[]{:S(2)}) async-start(bf16[8,32,256]{2,1,0:T(8,128)(2,1)} %bitcast.18), calls=%async_computation.5 | async-start | bytes 262144 | tf_op jit(solution)/shard_map/all_to_all | solution.py:51
  127.8 6.2 %all-to-all-done.4 = bf16[8,32,256]{2,1,0:T(8,128)(2,1)S(1)} async-done(((bf16[8,32,256]{2,1,0:T(8,128)(2,1)}), bf16[8,32,256]{2,1,0:T(8,128)(2,1)S(1)}, u32[]{:S(2)}, u32[]{:S(2)}) %all-to-all-start.4) | async-done | bytes 131104 | tf_op jit(solution)/shard_map/all_to_all | solution.py:51
  136.0 1.2 fusion.37
  137.2 71.5 %all-reduce.7.cloned.1.call-done = (f32[128,256]{0,1:T(8,128)}, f32[512,256]{1,0:T(8,128)}, f32[256,128]{1,0:T(8,128)}) async-done(((f32[128,256]{0,1:T(8,128)}, f32[512,256]{1,0:T(8,128)}, f32[256,128]{1,0:T(8,128)}), (f32[128,256]{0,1:T(8,128)}, f32[512,256]{1,0:T(8,128)}, f32[256,128]{1,0:T(8,128)})) %all-reduce.7.cloned.1.call-update) | async-done | bytes 786448 | tf_op jit(solution)/shard_map/psum | solution.py:199
  208.8 1.7 copy.24
  210.4 18.0 %all-reduce.5.cloned.1.call-done = f32[128,128]{1,0:T(8,128)} async-done(((f32[128,128]{1,0:T(8,128)}), f32[128,128]{1,0:T(8,128)}) %all-reduce.5.cloned.1.call-update) | async-done | bytes 65552 | tf_op jit(solution)/shard_map/psum | solution.py:147
  228.4 1.5 copy.29
  229.9 1.9 copy.30
  (92 shorter events, 19.8 us)
Async XLA Ops:
  7.2 90.0 %copy-start = (bf16[512,256]{1,0:T(8,128)(2,1)S(1)}, bf16[512,256]{1,0:T(8,128)(2,1)}, u32[]{:S(2)}) copy-start(bf16[512,256]{1,0:T(8,128)(2,1)} %param.17) | copy-start | bytes 786436
  7.2 0.7 copy-start.7
  8.1 0.7 copy-start.9
  8.1 8.8 %copy-start.8 = (s32[32,8]{0,1:T(8,128)S(1)}, s32[32,8]{0,1:T(8,128)}, u32[]{:S(2)}) copy-start(s32[32,8]{0,1:T(8,128)} %param.13) | copy-start | bytes 3076
  8.8 12.3 %copy-start.6 = (bf16[128,256]{1,0:T(8,128)(2,1)S(1)}, bf16[128,256]{1,0:T(8,128)(2,1)}, u32[]{:S(2)}) copy-start(bf16[128,256]{1,0:T(8,128)(2,1)} %param.15) | copy-start | bytes 196612
  9.6 19.2 %all-to-all-start = ((s32[8,1,32]{2,1,0:T(1,128)}), s32[8,1,32]{2,1,0:T(1,128)S(1)}, u32[]{:S(2)}, u32[]{:S(2)}) async-start(s32[8,1,32]{2,1,0:T(1,128)} %sub.20), calls=%async_computation | async-start | bytes 8192 | tf_op jit(solution)/shard_map/all_to_all | solution.py:33
  16.9 4.2 %copy-start.4 = (bf16[128,128]{1,0:T(8,128)(2,1)S(1)}, bf16[128,128]{1,0:T(8,128)(2,1)}, u32[]{:S(2)}) copy-start(bf16[128,128]{1,0:T(8,128)(2,1)} %param.10) | copy-start | bytes 98308
  17.1 8.5 %collective-permute-start.5 = (bf16[2,8,25]{2,1,0:T(8,128)(2,1)S(1)}, bf16[2,8,25]{2,1,0:T(8,128)(2,1)S(1)}, u32[]{:S(2)}, u32[]{:S(2)}) collective-permute-start(bf16[2,8,25]{2,1,0:T(8,128)(2,1)S(1)} %bitcast.73), channel_id=1, source_target_pairs={{4,0},{8,4},{12,8},{0,12},{5,1},{9,5},{13,9},{1,13},{6,2},{10,6},{... | collective-permute-start | bytes 2408 | tf_op jit(solution)/shard_map/ppermute | solution.py:19
  21.0 5.4 %collective-permute-start.4 = (bf16[2,8,25]{2,1,0:T(8,128)(2,1)S(1)}, bf16[2,8,25]{2,1,0:T(8,128)(2,1)S(1)}, u32[]{:S(2)}, u32[]{:S(2)}) collective-permute-start(bf16[2,8,25]{2,1,0:T(8,128)(2,1)S(1)} %bitcast.74), channel_id=1, source_target_pairs={{0,4},{4,8},{8,12},{12,0},{1,5},{5,9},{9,13},{13,1},{2,6},{6,10},{... | collective-permute-start | bytes 2408 | tf_op jit(solution)/shard_map/ppermute | solution.py:18
  21.3 0.9 copy-start.2
  21.3 0.9 copy-start.3
  22.2 1.1 copy-start.1
  26.5 7.6 %collective-permute-start.6 = (bf16[8,2,25]{2,1,0:T(2,128)(2,1)S(1)}, bf16[8,2,25]{2,1,0:T(2,128)(2,1)S(1)}, u32[]{:S(2)}, u32[]{:S(2)}) collective-permute-start(bf16[8,2,25]{2,1,0:T(2,128)(2,1)S(1)} %get-tuple-element.91), channel_id=1, source_target_pairs={{2,0},{0,2},{3,1},{1,3},{6,4},{4,6},{7,5},{5,7},{10,8},{8,10},{11,... | collective-permute-start | bytes 2408 | tf_op jit(solution)/shard_map/ppermute | solution.py:19
  28.0 6.1 %collective-permute-start.10 = (bf16[8,2,25]{2,1,0:T(2,128)(2,1)S(1)}, bf16[8,2,25]{2,1,0:T(2,128)(2,1)S(1)}, u32[]{:S(2)}, u32[]{:S(2)}) collective-permute-start(bf16[8,2,25]{2,1,0:T(2,128)(2,1)S(1)} %get-tuple-element.92), channel_id=1, source_target_pairs={{0,2},{2,0},{1,3},{3,1},{4,6},{6,4},{5,7},{7,5},{8,10},{10,8},{9,1... | collective-permute-start | bytes 2408 | tf_op jit(solution)/shard_map/ppermute | solution.py:18
  28.8 12.6 %all-to-all-start.1 = ((bf16[8,32,256]{2,1,0:T(8,128)(2,1)}), bf16[8,32,256]{2,1,0:T(8,128)(2,1)S(1)}, u32[]{:S(2)}, u32[]{:S(2)}) async-start(bf16[8,32,256]{2,1,0:T(8,128)(2,1)} %bitcast.1), calls=%async_computation.1 | async-start | bytes 262144 | tf_op jit(solution)/shard_map/all_to_all | solution.py:32
  41.4 10.7 %all-to-all-start.3 = ((bf16[8,32,256]{2,1,0:T(8,128)(2,1)}), bf16[8,32,256]{2,1,0:T(8,128)(2,1)S(1)}, u32[]{:S(2)}, u32[]{:S(2)}) async-start(bf16[8,32,256]{2,1,0:T(8,128)(2,1)} %bitcast.10), calls=%async_computation.3 | async-start | bytes 262144 | tf_op jit(solution)/shard_map/all_to_all | solution.py:47
  44.8 58.5 %reduce-scatter.2.cloned.1.call-start = ((), (), s32[]{:S(2)}) async-start(), calls=%async_computation.7 | async-start | bytes 49152 | tf_op jit(solution)/shard_map/reduce_scatter | solution.py:162
  45.1 7.3 %collective-permute-start.1 = (bf16[2,8,256]{2,1,0:T(8,128)(2,1)S(1)}, bf16[2,8,256]{2,1,0:T(8,128)(2,1)S(1)}, u32[]{:S(2)}, u32[]{:S(2)}) collective-permute-start(bf16[2,8,256]{2,1,0:T(8,128)(2,1)S(1)} %get-tuple-element.96), channel_id=1, source_target_pairs={{4,0},{8,4},{12,8},{0,12},{5,1},{9,5},{13,9},{1,13},{6,2},{10,6},{... | collective-permute-start | bytes 24584 | tf_op jit(solution)/shard_map/ppermute | solution.py:19
  48.8 5.4 %collective-permute-start = (bf16[2,8,256]{2,1,0:T(8,128)(2,1)S(1)}, bf16[2,8,256]{2,1,0:T(8,128)(2,1)S(1)}, u32[]{:S(2)}, u32[]{:S(2)}) collective-permute-start(bf16[2,8,256]{2,1,0:T(8,128)(2,1)S(1)} %get-tuple-element.95), channel_id=1, source_target_pairs={{0,4},{4,8},{8,12},{12,0},{1,5},{5,9},{9,13},{13,1},{2,6},{6,10},{... | collective-permute-start | bytes 24584 | tf_op jit(solution)/shard_map/ppermute | solution.py:18
  54.3 2.1 copy-start.10
  54.3 3.7 %collective-permute-start.2 = (bf16[8,2,256]{2,1,0:T(2,128)(2,1)S(1)}, bf16[8,2,256]{2,1,0:T(2,128)(2,1)S(1)}, u32[]{:S(2)}, u32[]{:S(2)}) collective-permute-start(bf16[8,2,256]{2,1,0:T(2,128)(2,1)S(1)} %get-tuple-element.87), channel_id=1, source_target_pairs={{0,2},{2,0},{1,3},{3,1},{4,6},{6,4},{5,7},{7,5},{8,10},{10,8},{9,1... | collective-permute-start | bytes 24584 | tf_op jit(solution)/shard_map/ppermute | solution.py:18
  55.9 3.7 %collective-permute-start.3 = (bf16[8,2,256]{2,1,0:T(2,128)(2,1)S(1)}, bf16[8,2,256]{2,1,0:T(2,128)(2,1)S(1)}, u32[]{:S(2)}, u32[]{:S(2)}) collective-permute-start(bf16[8,2,256]{2,1,0:T(2,128)(2,1)S(1)} %get-tuple-element.88), channel_id=1, source_target_pairs={{2,0},{0,2},{3,1},{1,3},{6,4},{4,6},{7,5},{5,7},{10,8},{8,10},{11,... | collective-permute-start | bytes 24584 | tf_op jit(solution)/shard_map/ppermute | solution.py:19
  106.4 8.8 %collective-permute-start.7 = (bf16[2,8,256]{2,1,0:T(8,128)(2,1)S(1)}, bf16[2,8,256]{2,1,0:T(8,128)(2,1)S(1)}, u32[]{:S(2)}, u32[]{:S(2)}) collective-permute-start(bf16[2,8,256]{2,1,0:T(8,128)(2,1)S(1)} %get-tuple-element.94), channel_id=1, source_target_pairs={{0,4},{4,8},{8,12},{12,0},{1,5},{5,9},{9,13},{13,1},{2,6},{6,10},{... | collective-permute-start | bytes 24584 | tf_op jit(solution)/shard_map/ppermute | solution.py:18
  108.2 7.1 %collective-permute-start.8 = (bf16[2,8,256]{2,1,0:T(8,128)(2,1)S(1)}, bf16[2,8,256]{2,1,0:T(8,128)(2,1)S(1)}, u32[]{:S(2)}, u32[]{:S(2)}) collective-permute-start(bf16[2,8,256]{2,1,0:T(8,128)(2,1)S(1)} %get-tuple-element.93), channel_id=1, source_target_pairs={{4,0},{8,4},{12,8},{0,12},{5,1},{9,5},{13,9},{1,13},{6,2},{10,6},{... | collective-permute-start | bytes 24584 | tf_op jit(solution)/shard_map/ppermute | solution.py:19
  111.3 11.3 %all-to-all-start.2 = ((bf16[8,32,256]{2,1,0:T(8,128)(2,1)}), bf16[8,32,256]{2,1,0:T(8,128)(2,1)S(1)}, u32[]{:S(2)}, u32[]{:S(2)}) async-start(bf16[8,32,256]{2,1,0:T(8,128)(2,1)} %bitcast.8), calls=%async_computation.2 | async-start | bytes 262144 | tf_op jit(solution)/shard_map/all_to_all | solution.py:43
  115.3 4.0 %collective-permute-start.9 = (bf16[8,2,256]{2,1,0:T(2,128)(2,1)S(1)}, bf16[8,2,256]{2,1,0:T(2,128)(2,1)S(1)}, u32[]{:S(2)}, u32[]{:S(2)}) collective-permute-start(bf16[8,2,256]{2,1,0:T(2,128)(2,1)S(1)} %get-tuple-element.83), channel_id=1, source_target_pairs={{2,0},{0,2},{3,1},{1,3},{6,4},{4,6},{7,5},{5,7},{10,8},{8,10},{11,... | collective-permute-start | bytes 24584 | tf_op jit(solution)/shard_map/ppermute | solution.py:19
  117.4 3.9 %collective-permute-start.11 = (bf16[8,2,256]{2,1,0:T(2,128)(2,1)S(1)}, bf16[8,2,256]{2,1,0:T(2,128)(2,1)S(1)}, u32[]{:S(2)}, u32[]{:S(2)}) collective-permute-start(bf16[8,2,256]{2,1,0:T(2,128)(2,1)S(1)} %get-tuple-element.84), channel_id=1, source_target_pairs={{0,2},{2,0},{1,3},{3,1},{4,6},{6,4},{5,7},{7,5},{8,10},{10,8},{9,1... | collective-permute-start | bytes 24584 | tf_op jit(solution)/shard_map/ppermute | solution.py:18
  122.6 11.4 %all-to-all-start.4 = ((bf16[8,32,256]{2,1,0:T(8,128)(2,1)}), bf16[8,32,256]{2,1,0:T(8,128)(2,1)S(1)}, u32[]{:S(2)}, u32[]{:S(2)}) async-start(bf16[8,32,256]{2,1,0:T(8,128)(2,1)} %bitcast.18), calls=%async_computation.5 | async-start | bytes 262144 | tf_op jit(solution)/shard_map/all_to_all | solution.py:51
  126.6 82.1 %all-reduce.7.cloned.1.call-start = ((), (), s32[]{:S(2)}) async-start(), calls=%async_computation.8 | async-start | bytes 1572864 | tf_op jit(solution)/shard_map/psum | solution.py:199
  135.2 93.2 %all-reduce.5.cloned.1.call-start = ((), (), s32[]{:S(2)}) async-start(), calls=%async_computation.6 | async-start | bytes 131072 | tf_op jit(solution)/shard_map/psum | solution.py:147
  229.9 1.9 copy-start.5
Sparse Core Ops, SparseCore 0:
  98.4 4.7 reduce-scatter.1
  135.3 73.4 all-reduce.6
  211.6 16.7 all-reduce.4
where the time goes:
time: 240 us; the launch traced here: 239 us
  waiting for transfers between devices  118 us (49%)
  starting transfers between devices  41.8 us (17%)
  blocking collectives  41.1 us (17%)
  between operations  14 us (6%)
  matrix products  13.2 us (6%)
  local copies, waits for them, and re-layouts  8.52 us (4%)
  other arithmetic  2.47 us (1%)
    psum x1, waiting for transfers between devices, body(): lax.psum((encode_grad, process_grad, decode_grad), ('mesh', 'tile'))  71.5 us
    psum x1, blocking collectives, body(): coarse_total = lax.psum(coarse_part, ('mesh', 'tile'))  33.4 us
    psum x1, waiting for transfers between devices, body(): prediction = lax.psum(pred_part, 'feat')  18 us
    ppermute x6, starting transfers between devices, padded(): after = lax.ppermute(initial, axis, down)  13.9 us
    all_to_all x3, starting transfers between devices, route_block(): lax.all_to_all(block.reshape(flat_shape), ('mesh', 'tile'), split_axis=0,...  11.3 us
    all_to_all x3, waiting for transfers between devices, route_block(): lax.all_to_all(block.reshape(flat_shape), ('mesh', 'tile'), split_axis=0,...  9.73 us
    all_to_all x1, starting transfers between devices, send_rows(): lax.all_to_all(slot_node, ('mesh', 'tile'), split_axis=0, concat_axis=0,...  7.28 us
    unnamed x26, local copies, waits for them, and re-layouts  6.89 us
  transfers between devices with their start and end apart: 20, of which 13 were waited for; matrix products, arithmetic and copies ran while one was open for 6% of the time, Pallas kernels for 0%

commit v1 on v0

--- a/solution.py
+++ b/solution.py
@@ -1,11 +1,275 @@
+import functools
+
 import jax
 import jax.numpy as jnp
 from jax import lax
+from jax.experimental import pallas as pl
+from jax.experimental.pallas import tpu as pltpu
 from jax.sharding import PartitionSpec as P
 
 MA = 4
 MB = 8
 CPD = 2
+ID_ROWS = 16
+REPLICATE_LIMIT = 1 << 20
+
+F32 = jnp.float32
+BF16 = jnp.bfloat16
+NN = (((1,), (0,)), ((), ()))
+NT = (((1,), (1,)), ((), ()))
+TN = (((0,), (0,)), ((), ()))
+
+
+def mm(lhs, rhs, dims=NN):
+    return lax.dot_general(lhs, rhs, dims, preferred_element_type=F32)
+
+
+def split(value):
+    high = value.astype(BF16)
+    return high, (value - high.astype(F32)).astype(BF16)
+
+
+def pack_kernel(fields, group_col, node_row, codes, coarse_row, cotangent, out, wide):
+    rows = fields.shape[0]
+    local, degree = codes.shape
+    core = lax.axis_index("feat")
+
+    @pl.when(core == 0)
+    def _():
+        out[0:rows, :] = fields[...]
+
+    @pl.when(core != 0)
+    def _():
+        out[0:rows, :] = cotangent[...].astype(BF16)
+
+    wide[...] = jnp.zeros(wide.shape, F32)
+    wide[:, 0:1] = group_col[...].astype(F32)
+    wide[0:local, 2 : 2 + degree] = codes[...].astype(F32)
+    turned = jnp.transpose(wide[...])
+    wide[0:ID_ROWS, :] = turned[0:ID_ROWS, :]
+    wide[1:2, :] = node_row[...].astype(F32)
+    wide[2 + degree : 3 + degree, 0:local] = coarse_row[...].astype(F32)
+    out[rows : rows + ID_ROWS, :] = wide[0:ID_ROWS, :].astype(BF16)
+
+
+def step_kernel(
+    mesh_count,
+    tile_count,
+    degree,
+    near,
+    far,
+    we_own,
+    wp_own,
+    wc_own,
+    wd_own,
+    we_oth,
+    wp_oth,
+    wc_oth,
+    wd_oth,
+    prediction,
+    encode_grad,
+    process_grad,
+    coarse_grad,
+    decode_grad,
+    cells,
+    cots,
+    hid,
+    slope,
+    hit,
+    hit_t,
+    ids,
+    gpe,
+):
+    groups = mesh_count * tile_count
+    local = MA * MB
+    nodes = groups * local
+    block = near.shape[0] // groups
+    rows = block - ID_ROWS
+    width = we_own.shape[1]
+    core = lax.axis_index("feat")
+    my_mesh = lax.axis_index("mesh")
+    my_tile = lax.axis_index("tile")
+    own = pl.ds(pl.multiple_of(core * width, width), width)
+    oth = pl.ds(pl.multiple_of((1 - core) * width, width), width)
+    sub = lax.broadcasted_iota(jnp.int32, (nodes, rows), 0).astype(F32)
+    lane = lax.broadcasted_iota(jnp.int32, (rows, nodes), 1).astype(F32)
+    for p in range(groups):
+        far_tile, shift = p // mesh_count, p % mesh_count
+        group = lax.rem(my_mesh - shift + mesh_count, mesh_count) * tile_count + lax.rem(
+            my_tile - far_tile + tile_count, tile_count
+        )
+        here = pl.ds(p * block, rows)
+        span = slice(p * rows, (p + 1) * rows)
+        a, b = near[here, :], far[here, :]
+        cell = jnp.where(core == 0, a, b)
+        cells[span, :] = cell
+        cots[span, :] = jnp.where(core == 0, b, a)
+        tags = near[pl.ds(p * block + rows, ID_ROWS), :].astype(F32)
+        tags_t = jnp.transpose(tags)
+        hit[:, span] = (sub == tags[0:1, :] * local + tags[1:2, :]).astype(BF16)
+        hit_t[span, :] = (lane == tags_t[:, 0:1] * local + tags_t[:, 1:2]).astype(BF16)
+        ids[pl.ds(pl.multiple_of(group * local, local), local), :] = tags_t[0:local, :]
+        pre = mm(cell, we_own[...])
+        sig = jax.nn.sigmoid(pre)
+        act = pre * sig
+        hid[span, 0:width] = act.astype(BF16)
+        slope[span, :] = sig + act * (1.0 - sig)
+        pre = mm(cell, we_oth[...])
+        hid[span, width:] = (pre * jax.nn.sigmoid(pre)).astype(BF16)
+
+    tags = ids[...].astype(jnp.int32)
+    index = lax.broadcasted_iota(jnp.int32, (nodes, ID_ROWS), 0)
+    group, place = lax.div(index, local), lax.rem(index, local)
+    row = lax.div(group, tile_count) * MA + lax.div(place, MB)
+    col = lax.rem(group, tile_count) * MB + lax.rem(place, MB)
+    tall, broad = mesh_count * MA, tile_count * MB
+    row = lax.rem(row + lax.div(tags, 5) - 2 + tall, tall)
+    col = lax.rem(col + lax.rem(tags, 5) - 2 + broad, broad)
+    peer = (lax.div(row, MA) * tile_count + lax.div(col, MB)) * local
+    peer = peer + lax.rem(row, MA) * MB + lax.rem(col, MB)
+    over = lax.broadcasted_iota(jnp.int32, (nodes, nodes), 1)
+    reach = jnp.zeros((nodes, nodes), F32)
+    for k in range(2, 2 + degree):
+        reach = reach + (over == peer[:, k : k + 1]).astype(F32)
+    reach = reach.astype(BF16)
+    coarse_count = CPD * groups
+    member = (
+        lax.broadcasted_iota(jnp.int32, (nodes, coarse_count), 1)
+        == tags[:, 2 + degree : 3 + degree]
+    ).astype(BF16)
+
+    node_in = mm(hit[...], hid[...]).astype(BF16)
+    agg = mm(reach, node_in).astype(BF16)
+    agg_own, agg_oth = agg[:, :width], agg[:, width:]
+    pre_mesh = (
+        mm(agg_own, wp_own[own, :]) + mm(agg_oth, wp_own[oth, :]),
+        mm(agg_own, wp_oth[own, :]) + mm(agg_oth, wp_oth[oth, :]),
+    )
+    sig_mesh = tuple(jax.nn.sigmoid(v) for v in pre_mesh)
+    act_mesh = tuple(v * s for v, s in zip(pre_mesh, sig_mesh))
+    level_one = (
+        node_in[:, :width].astype(F32) + act_mesh[0],
+        node_in[:, width:].astype(F32) + act_mesh[1],
+    )
+    coarse_in = []
+    for v in level_one:
+        high, low = split(v)
+        coarse_in.append((mm(member, high, TN) + mm(member, low, TN)).astype(BF16))
+    pre_coarse = (
+        mm(coarse_in[0], wc_own[own, :]) + mm(coarse_in[1], wc_own[oth, :]),
+        mm(coarse_in[0], wc_oth[own, :]) + mm(coarse_in[1], wc_oth[oth, :]),
+    )
+    sig_coarse = tuple(jax.nn.sigmoid(v) for v in pre_coarse)
+    act_coarse = tuple(v * s for v, s in zip(pre_coarse, sig_coarse))
+    level_two = tuple(
+        (v + mm(member, c.astype(BF16))).astype(BF16) for v, c in zip(level_one, act_coarse)
+    )
+    mine = hit_t[0:rows, :]
+    merged = (
+        (hid[0:rows, :width].astype(F32) + mm(mine, level_two[0])).astype(BF16),
+        (hid[0:rows, width:].astype(F32) + mm(mine, level_two[1])).astype(BF16),
+    )
+    prediction[...] = mm(merged[0], wd_own[...]) + mm(merged[1], wd_oth[...])
+
+    cot = cots[...]
+    node_cot = mm(hit[...], cot)
+    cot_high, cot_low = split(node_cot)
+    decode_grad[...] = mm(hid[:, :width], cot, TN) + mm(level_two[0], cot_high, TN)
+    grad_two = tuple(mm(cot_high, w[...], NT) + mm(cot_low, w[...], NT) for w in (wd_own, wd_oth))
+    grad_pre_coarse = []
+    for g, s, c in zip(grad_two, sig_coarse, act_coarse):
+        high, low = split(g)
+        total = mm(member, high, TN) + mm(member, low, TN)
+        grad_pre_coarse.append(total * (s + c * (1.0 - s)))
+    gpc = [v.astype(BF16) for v in grad_pre_coarse]
+    coarse_grad[own, :] = mm(coarse_in[0], gpc[0], TN)
+    coarse_grad[oth, :] = mm(coarse_in[1], gpc[0], TN)
+    grad_coarse_in = (
+        mm(gpc[0], wc_own[own, :], NT) + mm(gpc[1], wc_oth[own, :], NT),
+        mm(gpc[0], wc_own[oth, :], NT) + mm(gpc[1], wc_oth[oth, :], NT),
+    )
+    grad_one = tuple(g + mm(member, c.astype(BF16)) for g, c in zip(grad_two, grad_coarse_in))
+    gpm = tuple(
+        (g * (s + c * (1.0 - s))).astype(BF16) for g, s, c in zip(grad_one, sig_mesh, act_mesh)
+    )
+    process_grad[own, :] = mm(agg_own, gpm[0], TN)
+    process_grad[oth, :] = mm(agg_oth, gpm[0], TN)
+    grad_agg = (mm(gpm[0], wp_own[own, :], NT) + mm(gpm[1], wp_oth[own, :], NT)).astype(BF16)
+    grad_zero = (grad_one[0] + mm(reach, grad_agg, TN)).astype(BF16)
+    for p in range(groups):
+        span = slice(p * rows, (p + 1) * rows)
+        grad_hidden = mm(cots[span, :], wd_own[...], NT) + mm(hit_t[span, :], grad_zero)
+        gpe[span, :] = (grad_hidden * slope[span, :]).astype(BF16)
+    encode_grad[...] = mm(cells[...], gpe[...], TN)
+
+
+def replicated(
+    fields,
+    owner_group,
+    owner_node,
+    stencil_codes,
+    coarse_ids,
+    encode_weight,
+    process_weight,
+    coarse_weight,
+    decode_weight,
+    cotangent,
+):
+    mesh_count = lax.axis_size("mesh")
+    tile_count = lax.axis_size("tile")
+    groups = mesh_count * tile_count
+    rows, c_in = fields.shape
+    c_out = cotangent.shape[1]
+    width = encode_weight.shape[1]
+    nodes = groups * MA * MB
+    block = rows + ID_ROWS
+    weights = (encode_weight, process_weight, coarse_weight, decode_weight)
+    swap = [(0, 1), (1, 0)]
+    others = tuple(lax.ppermute(w, "feat", swap) for w in weights)
+    payload = pl.pallas_call(
+        pack_kernel,
+        out_shape=jax.ShapeDtypeStruct((block, c_in), BF16),
+        scratch_shapes=[pltpu.VMEM((rows, c_in), F32)],
+    )(
+        fields,
+        owner_group,
+        owner_node.reshape(1, rows),
+        stencil_codes,
+        coarse_ids.reshape(1, MA * MB),
+        cotangent,
+    )
+    blocks = [payload]
+    for shift in range(1, mesh_count):
+        ring = [(i, (i + shift) % mesh_count) for i in range(mesh_count)]
+        blocks.append(lax.ppermute(payload, "mesh", ring))
+    column = jnp.concatenate(blocks, axis=0)
+    columns = [column]
+    for shift in range(1, tile_count):
+        ring = [(i, (i + shift) % tile_count) for i in range(tile_count)]
+        columns.append(lax.ppermute(column, "tile", ring))
+    near = jnp.concatenate(columns, axis=0)
+    far = lax.ppermute(near, "feat", swap)
+    cells = groups * rows
+    return pl.pallas_call(
+        functools.partial(step_kernel, mesh_count, tile_count, stencil_codes.shape[1]),
+        out_shape=(
+            jax.ShapeDtypeStruct((rows, c_out), F32),
+            jax.ShapeDtypeStruct((c_in, width), F32),
+            jax.ShapeDtypeStruct(process_weight.shape, F32),
+            jax.ShapeDtypeStruct(coarse_weight.shape, F32),
+            jax.ShapeDtypeStruct((width, c_out), F32),
+        ),
+        scratch_shapes=[
+            pltpu.VMEM((cells, c_in), BF16),
+            pltpu.VMEM((cells, c_out), BF16),
+            pltpu.VMEM((cells, 2 * width), BF16),
+            pltpu.VMEM((cells, width), F32),
+            pltpu.VMEM((nodes, cells), BF16),
+            pltpu.VMEM((cells, nodes), BF16),
+            pltpu.VMEM((nodes, ID_ROWS), F32),
+            pltpu.VMEM((cells, width), BF16),
+        ],
+    )(near, far, *weights, *others)
 
 
 def padded(array, sides, width):
@@ -54,7 +318,7 @@
     return moved.reshape(-1, feat_width)
 
 
-def body(
+def distributed(
     fields,
     owner_group,
     owner_node,
@@ -202,6 +466,23 @@
     return (prediction, encode_grad, process_grad, coarse_grad, decode_grad)
 
 
+def body(fields, owner_group, owner_node, stencil_codes, *rest):
+    groups = lax.axis_size("mesh") * lax.axis_size("tile")
+    rows, c_in = fields.shape
+    cells, nodes = groups * rows, groups * MA * MB
+    degree = stencil_codes.shape[1]
+    fits = (
+        cells * nodes <= REPLICATE_LIMIT
+        and lax.axis_size("feat") == 2
+        and rows == c_in == rest[-1].shape[1]
+        and max(nodes, 25) <= 256
+        and degree + 3 <= ID_ROWS
+        and MA * MB <= rows
+    )
+    plan = replicated if fits else distributed
+    return plan(fields, owner_group, owner_node, stencil_codes, *rest)
+
+
 def solution(mesh):
     placed = (
         P(("parts", "mesh", "tile"), None),

time: 240 us -> 32.5 us (0.14)
  waiting for transfers between devices: 118 us -> 9.15 us
  blocking collectives: 41.1 us -> 0 us
  starting transfers between devices: 41.8 us -> 8.8 us
  between operations: 14 us -> 0.75 us
  matrix products: 13.2 us -> 0 us
  Pallas kernels: 0 us -> 8.96 us
  local copies, waits for them, and re-layouts: 8.52 us -> 4.51 us
  other arithmetic: 2.47 us -> 0.01 us
    psum x2 -> x0, waiting for transfers between devices: 89.5 us -> none  [the longest x1 71.5 us: body(): lax.psum((encode_grad, process_grad, decode_grad), ('mesh', 'tile'))]
    psum x1 -> x0, blocking collectives: 33.4 us -> none  [body(): coarse_total = lax.psum(coarse_part, ('mesh', 'tile'))]
    all_to_all x5 -> x0, starting transfers between devices: 23.9 us -> none  [the longest x3 11.3 us: route_block(): lax.all_to_all(block.reshape(flat_shape), ('mesh', 'tile'), split_axis=0,...]
    all_to_all x5 -> x0, waiting for transfers between devices: 15.6 us -> none  [the longest x3 9.73 us: route_block(): lax.all_to_all(block.reshape(flat_shape), ('mesh', 'tile'), split_axis=0,...]
    dot_general x22 -> x0, matrix products: 13.2 us -> none  [the longest x1 1.21 us: body(): jnp.dot(agg_full.astype(jnp.float32).T, grad_pre_mesh, precision=highest)]
    ppermute x12 -> x9, starting transfers between devices: 17.8 us -> 8.8 us  [the longest x3 6.09 us: replicated(): blocks.append(lax.ppermute(payload, 'mesh', ring))]
    pallas_call x0 -> x2, Pallas kernels: none -> 8.96 us  [the longest x1 7.25 us: replicated(): pl.pallas_call(functools.partial(step_kernel, mesh_count, tile_count, ste...]
    all_gather x4 -> x0, blocking collectives: 7.66 us -> none  [the longest x1 2.17 us: body(): weight_full = lax.all_gather(process_weight, 'feat', axis=1, tiled=True)]
  transfers between devices with their start and end apart: 20 -> 9, of which waited for: 13 -> 6; matrix products, arithmetic and copies ran while one was open for 6% -> 3% of each run, Pallas kernels for 0% -> 0%
where the time goes in v1:
time: 32.5 us; the launch traced here: 32.2 us
  waiting for transfers between devices  9.15 us (28%)
  Pallas kernels  8.96 us (28%)
  starting transfers between devices  8.8 us (27%)
  local copies, waits for them, and re-layouts  4.51 us (14%)
  between operations  0.75 us (2%)
    pallas_call x1, Pallas kernels, replicated(): pl.pallas_call(functools.partial(step_kernel, mesh_count, tile_count, ste...  7.25 us
    ppermute x3, starting transfers between devices, replicated(): blocks.append(lax.ppermute(payload, 'mesh', ring))  6.09 us
    unnamed x30, local copies, waits for them, and re-layouts  4.49 us
    ppermute x3, waiting for transfers between devices, replicated(): blocks.append(lax.ppermute(payload, 'mesh', ring))  4.15 us
    ppermute x1, waiting for transfers between devices, replicated(): columns.append(lax.ppermute(column, 'tile', ring))  3.59 us
    pallas_call x1, Pallas kernels, replicated(): pl.pallas_call(pack_kernel, out_shape=jax.ShapeDtypeStruct((block, c_in),...  1.71 us
    ppermute x1, starting transfers between devices, replicated(): columns.append(lax.ppermute(column, 'tile', ring))  1.56 us
    ppermute x4, waiting for transfers between devices, replicated(): others = tuple((lax.ppermute(w, 'feat', swap) for w in weights))  1.4 us
  transfers between devices with their start and end apart: 9, of which 6 were waited for; matrix products, arithmetic and copies ran while one was open for 3% of the time, Pallas kernels for 0%

profile of v1, /device:TPU:0, one launch (start us, length us, event | category | flops | bytes accessed | tf_op | source)
XLA Modules:
  0.0 32.2 jit_solution(2905213988800908040)
XLA Ops:
  0.6 1.4 %copy.16.codes = s32[32,8]{1,0:T(8,128)} copy(s32[32,8]{0,1:T(8,128)} %param.13) | data formatting | bytes 2048 | tf_op args[3]
  2.0 0.0 copy-done.11
  2.0 0.7 %copy.15.group_col = s32[128,1]{1,0:T(8,128)} copy(s32[128,1]{0,1:T(1,128)S(1)} %copy-done.11) | data formatting | bytes 1024 | tf_op args[1]
  2.8 1.7 %shard_map.137 = bf16[144,128]{1,0:T(8,128)(2,1)} custom-call(bf16[128,128]{1,0:T(8,128)(2,1)} %fields.1, s32[128,1]{1,0:T(8,128)} %copy.15.group_col, s32[1,128]{1,0:T(1,128)} %bitcast.2, s32[32,8]{1,0:T(8,128)} %copy.16.codes, s32[1,32]{1,0:T(1,128)} %bitcast.3, f32[128,128]{1,0:T(8,128)} %cotangent.1), custom_call_target="tpu_custom_call" | custom-call | tf_op jit(solution)/shard_map/pallas_call | solution.py:229
  4.5 5.1 %collective-permute-start.2 = (bf16[144,128]{1,0:T(8,128)(2,1)}, bf16[144,128]{1,0:T(8,128)(2,1)S(1)}, u32[]{:S(2)}, u32[]{:S(2)}) collective-permute-start(bf16[144,128]{1,0:T(8,128)(2,1)} %shard_map.137), channel_id=1, source_target_pairs={{0,12},{4,0},{8,4},{12,8},{1,13},{5,1},{9,5},{13,9},{2,14},{6,2},{... | collective-permute-start | bytes 110600 | tf_op jit(solution)/shard_map/ppermute | solution.py:244
  9.5 0.0 collective-permute-start.1
  9.6 1.0 %collective-permute-start = (bf16[144,128]{1,0:T(8,128)(2,1)}, bf16[144,128]{1,0:T(8,128)(2,1)S(1)}, u32[]{:S(2)}, u32[]{:S(2)}) collective-permute-start(bf16[144,128]{1,0:T(8,128)(2,1)} %shard_map.137), channel_id=1, source_target_pairs={{0,4},{4,8},{8,12},{12,0},{1,5},{5,9},{9,13},{13,1},{2,6},{6,10},{... | collective-permute-start | bytes 110600 | tf_op jit(solution)/shard_map/ppermute | solution.py:244
  10.6 0.8 %constant_dynamic-update-slice_fusion.4 = bf16[1152,128]{1,0:T(8,128)(2,1)S(1)} fusion(bf16[144,128]{1,0:T(8,128)(2,1)} %shard_map.137), kind=kLoop, calls=%fused_computation.5 | loop fusion | bytes 73728
  11.4 0.1 collective-permute-done.2
  11.5 3.1 %collective-permute-done.1 = bf16[144,128]{1,0:T(8,128)(2,1)S(1)} collective-permute-done((bf16[144,128]{1,0:T(8,128)(2,1)}, bf16[144,128]{1,0:T(8,128)(2,1)S(1)}, u32[]{:S(2)}, u32[]{:S(2)}) %collective-permute-start.1) | collective-permute-done | bytes 36896 | tf_op jit(solution)/shard_map/ppermute | solution.py:244
  14.6 0.9 %collective-permute-done = bf16[144,128]{1,0:T(8,128)(2,1)S(1)} collective-permute-done((bf16[144,128]{1,0:T(8,128)(2,1)}, bf16[144,128]{1,0:T(8,128)(2,1)S(1)}, u32[]{:S(2)}, u32[]{:S(2)}) %collective-permute-start) | collective-permute-done | bytes 36896 | tf_op jit(solution)/shard_map/ppermute | solution.py:244
  15.5 0.0 copy-start.3
  15.6 1.6 %collective-permute-start.3 = (bf16[576,128]{1,0:T(8,128)(2,1)S(1)}, bf16[576,128]{1,0:T(8,128)(2,1)S(1)}, u32[]{:S(2)}, u32[]{:S(2)}) collective-permute-start(bf16[576,128]{1,0:T(8,128)(2,1)S(1)} %pad_maximum_fusion), channel_id=1, source_target_pairs={{0,2},{2,0},{1,3},{3,1},{4,6},{6,4},{5,7},{7,5},{8,10},{10,8},{9,1... | collective-permute-start | bytes 442376 | tf_op jit(solution)/shard_map/ppermute | solution.py:249
  17.1 0.0 copy-start.7
  17.2 0.0 copy-start.8
  17.2 3.6 %collective-permute-done.3 = bf16[576,128]{1,0:T(8,128)(2,1)S(1)} collective-permute-done((bf16[576,128]{1,0:T(8,128)(2,1)S(1)}, bf16[576,128]{1,0:T(8,128)(2,1)S(1)}, u32[]{:S(2)}, u32[]{:S(2)}) %collective-permute-start.3) | collective-permute-done | bytes 147488 | tf_op jit(solution)/shard_map/ppermute | solution.py:249
  20.8 0.1 collective-permute-start.4
  20.9 0.5 %collective-permute-start.6 = (bf16[512,256]{1,0:T(8,128)(2,1)S(1)}, bf16[512,256]{1,0:T(8,128)(2,1)S(1)}, u32[]{:S(2)}, u32[]{:S(2)}) collective-permute-start(bf16[512,256]{1,0:T(8,128)(2,1)S(1)} %copy-done.3), channel_id=1, source_target_pairs={{0,1},{1,0},{2,3},{3,2},{4,5},{5,4},{6,7},{7,6},{8,9},{9,8},{10,11... | collective-permute-start | bytes 786440 | tf_op jit(solution)/shard_map/ppermute | solution.py:228
  21.4 0.1 collective-permute-start.7
  21.5 0.4 %collective-permute-start.5 = (bf16[128,256]{1,0:T(8,128)(2,1)S(1)}, bf16[128,256]{1,0:T(8,128)(2,1)S(1)}, u32[]{:S(2)}, u32[]{:S(2)}) collective-permute-start(bf16[128,256]{1,0:T(8,128)(2,1)S(1)} %copy-done.7), channel_id=1, source_target_pairs={{0,1},{1,0},{2,3},{3,2},{4,5},{5,4},{6,7},{7,6},{8,9},{9,8},{10,11... | collective-permute-start | bytes 196616 | tf_op jit(solution)/shard_map/ppermute | solution.py:228
  21.9 0.1 collective-permute-start.8
  22.0 1.3 %collective-permute-done.5.we_oth = bf16[128,256]{1,0:T(8,128)(2,1)S(1)} collective-permute-done((bf16[128,256]{1,0:T(8,128)(2,1)S(1)}, bf16[128,256]{1,0:T(8,128)(2,1)S(1)}, u32[]{:S(2)}, u32[]{:S(2)}) %collective-permute-start.5) | collective-permute-done | bytes 65568 | tf_op jit(solution)/shard_map/ppermute | solution.py:228
  23.3 0.1 collective-permute-done.8.wd_oth
  23.4 0.0 collective-permute-done.6.wp_oth
  23.4 0.0 collective-permute-done.7.wc_oth
  23.4 0.0 collective-permute-done.4.far
  23.4 0.5 %copy-done.9 = bf16[128,256]{1,0:T(8,128)(2,1)} copy-done((bf16[128,256]{1,0:T(8,128)(2,1)}, bf16[128,256]{1,0:T(8,128)(2,1)S(1)}, u32[]{:S(2)}) %copy-start.9) | copy-done | bytes 65560
  23.9 0.1 copy-done.10
  24.0 0.1 copy-done.5
  24.1 0.1 copy-done.6
  24.2 0.7 %copy-done.2 = bf16[1152,128]{1,0:T(8,128)(2,1)} copy-done((bf16[1152,128]{1,0:T(8,128)(2,1)}, bf16[1152,128]{1,0:T(8,128)(2,1)S(1)}, u32[]{:S(2)}) %copy-start.2) | copy-done | bytes 294936
  24.9 7.3 %shard_map.138 = (f32[128,128]{1,0:T(8,128)}, f32[128,256]{1,0:T(8,128)}, f32[512,256]{1,0:T(8,128)}, f32[512,256]{1,0:T(8,128)}, f32[256,128]{1,0:T(8,128)}) custom-call(bf16[1152,128]{1,0:T(8,128)(2,1)} %copy-done, bf16[1152,128]{1,0:T(8,128)(2,1)} %copy-done.2, bf16[128,256]{1,0:T(8,128)(2,1)} %we_own.1, bf16[512,256]{1,0:T(8,128)(2,1)} %wp_own.1, ...), custom_call_target="tpu_custom_call" | custom-call | tf_op jit(solution)/shard_map/pallas_call | solution.py:253
  (20 shorter events, 0.1 us)
Async XLA Ops:
  0.6 1.4 %copy-start.11 = (s32[128,1]{0,1:T(1,128)S(1)}, s32[128,1]{0,1:T(1,128)}, u32[]{:S(2)}) copy-start(s32[128,1]{0,1:T(1,128)} %param.11) | copy-start | bytes 1540
  4.5 11.1 %copy-start.1 = (bf16[144,128]{1,0:T(8,128)(2,1)S(1)}, bf16[144,128]{1,0:T(8,128)(2,1)}, u32[]{:S(2)}) copy-start(bf16[144,128]{1,0:T(8,128)(2,1)} %shard_map.137) | copy-start | bytes 110596
  4.5 7.0 %collective-permute-start.2 = (bf16[144,128]{1,0:T(8,128)(2,1)}, bf16[144,128]{1,0:T(8,128)(2,1)S(1)}, u32[]{:S(2)}, u32[]{:S(2)}) collective-permute-start(bf16[144,128]{1,0:T(8,128)(2,1)} %shard_map.137), channel_id=1, source_target_pairs={{0,12},{4,0},{8,4},{12,8},{1,13},{5,1},{9,5},{13,9},{2,14},{6,2},{... | collective-permute-start | bytes 110600 | tf_op jit(solution)/shard_map/ppermute | solution.py:244
  9.5 5.1 %collective-permute-start.1 = (bf16[144,128]{1,0:T(8,128)(2,1)}, bf16[144,128]{1,0:T(8,128)(2,1)S(1)}, u32[]{:S(2)}, u32[]{:S(2)}) collective-permute-start(bf16[144,128]{1,0:T(8,128)(2,1)} %shard_map.137), channel_id=1, source_target_pairs={{0,8},{4,12},{8,0},{12,4},{1,9},{5,13},{9,1},{13,5},{2,10},{6,14},... | collective-permute-start | bytes 110600 | tf_op jit(solution)/shard_map/ppermute | solution.py:244
  9.6 6.0 %collective-permute-start = (bf16[144,128]{1,0:T(8,128)(2,1)}, bf16[144,128]{1,0:T(8,128)(2,1)S(1)}, u32[]{:S(2)}, u32[]{:S(2)}) collective-permute-start(bf16[144,128]{1,0:T(8,128)(2,1)} %shard_map.137), channel_id=1, source_target_pairs={{0,4},{4,8},{8,12},{12,0},{1,5},{5,9},{9,13},{13,1},{2,6},{6,10},{... | collective-permute-start | bytes 110600 | tf_op jit(solution)/shard_map/ppermute | solution.py:244
  15.5 5.9 %copy-start.4 = (bf16[512,256]{1,0:T(8,128)(2,1)S(1)}, bf16[512,256]{1,0:T(8,128)(2,1)}, u32[]{:S(2)}) copy-start(bf16[512,256]{1,0:T(8,128)(2,1)} %wc_own.1) | copy-start | bytes 786436
  15.5 5.3 %copy-start.3 = (bf16[512,256]{1,0:T(8,128)(2,1)S(1)}, bf16[512,256]{1,0:T(8,128)(2,1)}, u32[]{:S(2)}) copy-start(bf16[512,256]{1,0:T(8,128)(2,1)} %wp_own.1) | copy-start | bytes 786436
  15.6 5.2 %collective-permute-start.3 = (bf16[576,128]{1,0:T(8,128)(2,1)S(1)}, bf16[576,128]{1,0:T(8,128)(2,1)S(1)}, u32[]{:S(2)}, u32[]{:S(2)}) collective-permute-start(bf16[576,128]{1,0:T(8,128)(2,1)S(1)} %pad_maximum_fusion), channel_id=1, source_target_pairs={{0,2},{2,0},{1,3},{3,1},{4,6},{6,4},{5,7},{7,5},{8,10},{10,8},{9,1... | collective-permute-start | bytes 442376 | tf_op jit(solution)/shard_map/ppermute | solution.py:249
  17.1 4.3 %copy-start.7 = (bf16[128,256]{1,0:T(8,128)(2,1)S(1)}, bf16[128,256]{1,0:T(8,128)(2,1)}, u32[]{:S(2)}) copy-start(bf16[128,256]{1,0:T(8,128)(2,1)} %we_own.1) | copy-start | bytes 196612
  17.2 4.7 %copy-start.8 = (bf16[256,128]{1,0:T(8,128)(2,1)S(1)}, bf16[256,128]{1,0:T(8,128)(2,1)}, u32[]{:S(2)}) copy-start(bf16[256,128]{1,0:T(8,128)(2,1)} %wd_own.1) | copy-start | bytes 196612
  20.8 2.6 %copy-start = (bf16[1152,128]{1,0:T(8,128)(2,1)}, bf16[1152,128]{1,0:T(8,128)(2,1)S(1)}, u32[]{:S(2)}) copy-start(bf16[1152,128]{1,0:T(8,128)(2,1)S(1)} %constant_dynamic-update-slice_fusion.near) | copy-start | bytes 884740
  20.8 2.6 %collective-permute-start.4 = (bf16[1152,128]{1,0:T(8,128)(2,1)S(1)}, bf16[1152,128]{1,0:T(8,128)(2,1)S(1)}, u32[]{:S(2)}, u32[]{:S(2)}) collective-permute-start(bf16[1152,128]{1,0:T(8,128)(2,1)S(1)} %constant_dynamic-update-slice_fusion.near), channel_id=1, source_target_pairs={{0,1},{1,0},{2,3},{3,2},{4,5},{5,4},{6,7},{7,6},{8,9},{9,8},{10,11... | collective-permute-start | bytes 884744 | tf_op jit(solution)/shard_map/ppermute | solution.py:251
  20.9 2.5 %collective-permute-start.6 = (bf16[512,256]{1,0:T(8,128)(2,1)S(1)}, bf16[512,256]{1,0:T(8,128)(2,1)S(1)}, u32[]{:S(2)}, u32[]{:S(2)}) collective-permute-start(bf16[512,256]{1,0:T(8,128)(2,1)S(1)} %copy-done.3), channel_id=1, source_target_pairs={{0,1},{1,0},{2,3},{3,2},{4,5},{5,4},{6,7},{7,6},{8,9},{9,8},{10,11... | collective-permute-start | bytes 786440 | tf_op jit(solution)/shard_map/ppermute | solution.py:228
  21.4 2.0 %collective-permute-start.7 = (bf16[512,256]{1,0:T(8,128)(2,1)S(1)}, bf16[512,256]{1,0:T(8,128)(2,1)S(1)}, u32[]{:S(2)}, u32[]{:S(2)}) collective-permute-start(bf16[512,256]{1,0:T(8,128)(2,1)S(1)} %copy-done.4), channel_id=1, source_target_pairs={{0,1},{1,0},{2,3},{3,2},{4,5},{5,4},{6,7},{7,6},{8,9},{9,8},{10,11... | collective-permute-start | bytes 786440 | tf_op jit(solution)/shard_map/ppermute | solution.py:228
  21.5 1.8 %collective-permute-start.5 = (bf16[128,256]{1,0:T(8,128)(2,1)S(1)}, bf16[128,256]{1,0:T(8,128)(2,1)S(1)}, u32[]{:S(2)}, u32[]{:S(2)}) collective-permute-start(bf16[128,256]{1,0:T(8,128)(2,1)S(1)} %copy-done.7), channel_id=1, source_target_pairs={{0,1},{1,0},{2,3},{3,2},{4,5},{5,4},{6,7},{7,6},{8,9},{9,8},{10,11... | collective-permute-start | bytes 196616 | tf_op jit(solution)/shard_map/ppermute | solution.py:228
  21.9 1.5 %collective-permute-start.8 = (bf16[256,128]{1,0:T(8,128)(2,1)S(1)}, bf16[256,128]{1,0:T(8,128)(2,1)S(1)}, u32[]{:S(2)}, u32[]{:S(2)}) collective-permute-start(bf16[256,128]{1,0:T(8,128)(2,1)S(1)} %copy-done.8), channel_id=1, source_target_pairs={{0,1},{1,0},{2,3},{3,2},{4,5},{5,4},{6,7},{7,6},{8,9},{9,8},{10,11... | collective-permute-start | bytes 196616 | tf_op jit(solution)/shard_map/ppermute | solution.py:228
  23.3 0.6 %copy-start.9 = (bf16[128,256]{1,0:T(8,128)(2,1)}, bf16[128,256]{1,0:T(8,128)(2,1)S(1)}, u32[]{:S(2)}) copy-start(bf16[128,256]{1,0:T(8,128)(2,1)S(1)} %collective-permute-done.5.we_oth) | copy-start | bytes 196612
  23.4 0.6 %copy-start.10 = (bf16[256,128]{1,0:T(8,128)(2,1)}, bf16[256,128]{1,0:T(8,128)(2,1)S(1)}, u32[]{:S(2)}) copy-start(bf16[256,128]{1,0:T(8,128)(2,1)S(1)} %collective-permute-done.8.wd_oth) | copy-start | bytes 196612
  23.4 0.7 %copy-start.5 = (bf16[512,256]{1,0:T(8,128)(2,1)}, bf16[512,256]{1,0:T(8,128)(2,1)S(1)}, u32[]{:S(2)}) copy-start(bf16[512,256]{1,0:T(8,128)(2,1)S(1)} %collective-permute-done.6.wp_oth) | copy-start | bytes 786436
  23.4 0.8 %copy-start.6 = (bf16[512,256]{1,0:T(8,128)(2,1)}, bf16[512,256]{1,0:T(8,128)(2,1)S(1)}, u32[]{:S(2)}) copy-start(bf16[512,256]{1,0:T(8,128)(2,1)S(1)} %collective-permute-done.7.wc_oth) | copy-start | bytes 786436
  24.2 0.7 %copy-start.2 = (bf16[1152,128]{1,0:T(8,128)(2,1)}, bf16[1152,128]{1,0:T(8,128)(2,1)S(1)}, u32[]{:S(2)}) copy-start(bf16[1152,128]{1,0:T(8,128)(2,1)S(1)} %collective-permute-done.4.far) | copy-start | bytes 884740

commit v2 on v1

--- a/solution.py
+++ b/solution.py
@@ -29,9 +29,13 @@
     return high, (value - high.astype(F32)).astype(BF16)
 
 
-def pack_kernel(fields, group_col, node_row, codes, coarse_row, cotangent, out, wide):
+def held(value):
+    return pltpu.with_memory_space_constraint(value, pltpu.VMEM)
+
+
+def pack_kernel(fields, group_row, node_row, codes, coarse_row, cotangent, out, wide):
     rows = fields.shape[0]
-    local, degree = codes.shape
+    degree, local = codes.shape
     core = lax.axis_index("feat")
 
     @pl.when(core == 0)
@@ -43,54 +47,21 @@
         out[0:rows, :] = cotangent[...].astype(BF16)
 
     wide[...] = jnp.zeros(wide.shape, F32)
-    wide[:, 0:1] = group_col[...].astype(F32)
-    wide[0:local, 2 : 2 + degree] = codes[...].astype(F32)
-    turned = jnp.transpose(wide[...])
-    wide[0:ID_ROWS, :] = turned[0:ID_ROWS, :]
+    wide[0:1, :] = group_row[...].astype(F32)
     wide[1:2, :] = node_row[...].astype(F32)
+    wide[2 : 2 + degree, 0:local] = codes[...].astype(F32)
     wide[2 + degree : 3 + degree, 0:local] = coarse_row[...].astype(F32)
-    out[rows : rows + ID_ROWS, :] = wide[0:ID_ROWS, :].astype(BF16)
-
-
-def step_kernel(
-    mesh_count,
-    tile_count,
-    degree,
-    near,
-    far,
-    we_own,
-    wp_own,
-    wc_own,
-    wd_own,
-    we_oth,
-    wp_oth,
-    wc_oth,
-    wd_oth,
-    prediction,
-    encode_grad,
-    process_grad,
-    coarse_grad,
-    decode_grad,
-    cells,
-    cots,
-    hid,
-    slope,
-    hit,
-    hit_t,
-    ids,
-    gpe,
-):
+    out[rows : rows + ID_ROWS, :] = wide[...].astype(BF16)
+
+
+def index_kernel(mesh_count, tile_count, degree, near, hit, hit_t, reach_out, member_out, ids):
     groups = mesh_count * tile_count
     local = MA * MB
     nodes = groups * local
     block = near.shape[0] // groups
     rows = block - ID_ROWS
-    width = we_own.shape[1]
-    core = lax.axis_index("feat")
     my_mesh = lax.axis_index("mesh")
     my_tile = lax.axis_index("tile")
-    own = pl.ds(pl.multiple_of(core * width, width), width)
-    oth = pl.ds(pl.multiple_of((1 - core) * width, width), width)
     sub = lax.broadcasted_iota(jnp.int32, (nodes, rows), 0).astype(F32)
     lane = lax.broadcasted_iota(jnp.int32, (rows, nodes), 1).astype(F32)
     for p in range(groups):
@@ -98,24 +69,12 @@
         group = lax.rem(my_mesh - shift + mesh_count, mesh_count) * tile_count + lax.rem(
             my_tile - far_tile + tile_count, tile_count
         )
-        here = pl.ds(p * block, rows)
         span = slice(p * rows, (p + 1) * rows)
-        a, b = near[here, :], far[here, :]
-        cell = jnp.where(core == 0, a, b)
-        cells[span, :] = cell
-        cots[span, :] = jnp.where(core == 0, b, a)
         tags = near[pl.ds(p * block + rows, ID_ROWS), :].astype(F32)
         tags_t = jnp.transpose(tags)
         hit[:, span] = (sub == tags[0:1, :] * local + tags[1:2, :]).astype(BF16)
         hit_t[span, :] = (lane == tags_t[:, 0:1] * local + tags_t[:, 1:2]).astype(BF16)
         ids[pl.ds(pl.multiple_of(group * local, local), local), :] = tags_t[0:local, :]
-        pre = mm(cell, we_own[...])
-        sig = jax.nn.sigmoid(pre)
-        act = pre * sig
-        hid[span, 0:width] = act.astype(BF16)
-        slope[span, :] = sig + act * (1.0 - sig)
-        pre = mm(cell, we_oth[...])
-        hid[span, width:] = (pre * jax.nn.sigmoid(pre)).astype(BF16)
 
     tags = ids[...].astype(jnp.int32)
     index = lax.broadcasted_iota(jnp.int32, (nodes, ID_ROWS), 0)
@@ -131,13 +90,81 @@
     reach = jnp.zeros((nodes, nodes), F32)
     for k in range(2, 2 + degree):
         reach = reach + (over == peer[:, k : k + 1]).astype(F32)
-    reach = reach.astype(BF16)
-    coarse_count = CPD * groups
-    member = (
-        lax.broadcasted_iota(jnp.int32, (nodes, coarse_count), 1)
+    reach_out[...] = reach.astype(BF16)
+    member_out[...] = (
+        lax.broadcasted_iota(jnp.int32, (nodes, CPD * groups), 1)
         == tags[:, 2 + degree : 3 + degree]
     ).astype(BF16)
 
+
+def step_kernel(
+    groups,
+    near,
+    far,
+    hit,
+    hit_t,
+    reach_ref,
+    member_ref,
+    we_own,
+    wp_own,
+    wc_own,
+    wd_own,
+    we_oth,
+    wp_oth,
+    wc_oth,
+    wd_oth,
+    prediction_out,
+    encode_out,
+    process_out,
+    coarse_out,
+    decode_out,
+    cells,
+    cots,
+    hid,
+    slope,
+    gpe,
+    prediction,
+    encode_grad,
+    process_grad,
+    coarse_grad,
+    decode_grad,
+    sems,
+):
+    block = near.shape[0] // groups
+    rows = block - ID_ROWS
+    width = we_own.shape[1]
+    core = lax.axis_index("feat")
+    own = pl.ds(pl.multiple_of(core * width, width), width)
+    oth = pl.ds(pl.multiple_of((1 - core) * width, width), width)
+    sent = [
+        pltpu.make_async_copy(source, target, sems.at[i])
+        for i, (source, target) in enumerate(
+            (
+                (prediction, prediction_out),
+                (encode_grad, encode_out),
+                (process_grad, process_out),
+                (coarse_grad, coarse_out),
+                (decode_grad, decode_out),
+            )
+        )
+    ]
+    for p in range(groups):
+        here = pl.ds(p * block, rows)
+        span = slice(p * rows, (p + 1) * rows)
+        a, b = near[here, :], far[here, :]
+        cell = jnp.where(core == 0, a, b)
+        cells[span, :] = cell
+        cots[span, :] = jnp.where(core == 0, b, a)
+        pre = mm(cell, we_own[...])
+        sig = jax.nn.sigmoid(pre)
+        act = pre * sig
+        hid[span, 0:width] = act.astype(BF16)
+        slope[span, :] = sig + act * (1.0 - sig)
+        pre = mm(cell, we_oth[...])
+        hid[span, width:] = (pre * jax.nn.sigmoid(pre)).astype(BF16)
+
+    reach = reach_ref[...]
+    member = member_ref[...]
     node_in = mm(hit[...], hid[...]).astype(BF16)
     agg = mm(reach, node_in).astype(BF16)
     agg_own, agg_oth = agg[:, :width], agg[:, width:]
@@ -170,11 +197,13 @@
         (hid[0:rows, width:].astype(F32) + mm(mine, level_two[1])).astype(BF16),
     )
     prediction[...] = mm(merged[0], wd_own[...]) + mm(merged[1], wd_oth[...])
+    sent[0].start()
 
     cot = cots[...]
     node_cot = mm(hit[...], cot)
     cot_high, cot_low = split(node_cot)
     decode_grad[...] = mm(hid[:, :width], cot, TN) + mm(level_two[0], cot_high, TN)
+    sent[4].start()
     grad_two = tuple(mm(cot_high, w[...], NT) + mm(cot_low, w[...], NT) for w in (wd_own, wd_oth))
     grad_pre_coarse = []
     for g, s, c in zip(grad_two, sig_coarse, act_coarse):
@@ -184,6 +213,7 @@
     gpc = [v.astype(BF16) for v in grad_pre_coarse]
     coarse_grad[own, :] = mm(coarse_in[0], gpc[0], TN)
     coarse_grad[oth, :] = mm(coarse_in[1], gpc[0], TN)
+    sent[3].start()
     grad_coarse_in = (
         mm(gpc[0], wc_own[own, :], NT) + mm(gpc[1], wc_oth[own, :], NT),
         mm(gpc[0], wc_own[oth, :], NT) + mm(gpc[1], wc_oth[oth, :], NT),
@@ -194,6 +224,7 @@
     )
     process_grad[own, :] = mm(agg_own, gpm[0], TN)
     process_grad[oth, :] = mm(agg_oth, gpm[0], TN)
+    sent[2].start()
     grad_agg = (mm(gpm[0], wp_own[own, :], NT) + mm(gpm[1], wp_oth[own, :], NT)).astype(BF16)
     grad_zero = (grad_one[0] + mm(reach, grad_agg, TN)).astype(BF16)
     for p in range(groups):
@@ -201,6 +232,9 @@
         grad_hidden = mm(cots[span, :], wd_own[...], NT) + mm(hit_t[span, :], grad_zero)
         gpe[span, :] = (grad_hidden * slope[span, :]).astype(BF16)
     encode_grad[...] = mm(cells[...], gpe[...], TN)
+    sent[1].start()
+    for copy in sent:
+        copy.wait()
 
 
 def replicated(
@@ -225,24 +259,30 @@
     block = rows + ID_ROWS
     weights = (encode_weight, process_weight, coarse_weight, decode_weight)
     swap = [(0, 1), (1, 0)]
-    others = tuple(lax.ppermute(w, "feat", swap) for w in weights)
+    vmem = pl.BlockSpec(memory_space=pltpu.VMEM)
+    hbm = pl.BlockSpec(memory_space=pl.ANY)
     payload = pl.pallas_call(
         pack_kernel,
-        out_shape=jax.ShapeDtypeStruct((block, c_in), BF16),
-        scratch_shapes=[pltpu.VMEM((rows, c_in), F32)],
+        in_specs=[vmem] * 6,
+        out_specs=vmem,
+        out_shape=pltpu.VMEM((block, c_in), BF16),
+        scratch_shapes=[pltpu.VMEM((ID_ROWS, rows), F32)],
     )(
         fields,
-        owner_group,
+        owner_group.reshape(1, rows),
         owner_node.reshape(1, rows),
-        stencil_codes,
+        stencil_codes.T,
         coarse_ids.reshape(1, MA * MB),
         cotangent,
     )
+    payload, weights = lax.optimization_barrier((payload, weights))
     blocks = [payload]
     for shift in range(1, mesh_count):
         ring = [(i, (i + shift) % mesh_count) for i in range(mesh_count)]
         blocks.append(lax.ppermute(payload, "mesh", ring))
+    others = tuple(lax.ppermute(w, "feat", swap) for w in weights)
     column = jnp.concatenate(blocks, axis=0)
+    column, others = lax.optimization_barrier((column, others))
     columns = [column]
     for shift in range(1, tile_count):
         ring = [(i, (i + shift) % tile_count) for i in range(tile_count)]
@@ -250,26 +290,41 @@
     near = jnp.concatenate(columns, axis=0)
     far = lax.ppermute(near, "feat", swap)
     cells = groups * rows
+    degree = stencil_codes.shape[1]
+    tables = pl.pallas_call(
+        functools.partial(index_kernel, mesh_count, tile_count, degree),
+        in_specs=[vmem],
+        out_specs=[vmem] * 4,
+        out_shape=(
+            pltpu.VMEM((nodes, cells), BF16),
+            pltpu.VMEM((cells, nodes), BF16),
+            pltpu.VMEM((nodes, nodes), BF16),
+            pltpu.VMEM((nodes, CPD * groups), BF16),
+        ),
+        scratch_shapes=[pltpu.VMEM((nodes, ID_ROWS), F32)],
+    )(held(near))
+    outs = (
+        jax.ShapeDtypeStruct((rows, c_out), F32),
+        jax.ShapeDtypeStruct((c_in, width), F32),
+        jax.ShapeDtypeStruct(process_weight.shape, F32),
+        jax.ShapeDtypeStruct(coarse_weight.shape, F32),
+        jax.ShapeDtypeStruct((width, c_out), F32),
+    )
     return pl.pallas_call(
-        functools.partial(step_kernel, mesh_count, tile_count, stencil_codes.shape[1]),
-        out_shape=(
-            jax.ShapeDtypeStruct((rows, c_out), F32),
-            jax.ShapeDtypeStruct((c_in, width), F32),
-            jax.ShapeDtypeStruct(process_weight.shape, F32),
-            jax.ShapeDtypeStruct(coarse_weight.shape, F32),
-            jax.ShapeDtypeStruct((width, c_out), F32),
-        ),
+        functools.partial(step_kernel, groups),
+        in_specs=[vmem] * 14,
+        out_specs=[hbm] * 5,
+        out_shape=outs,
         scratch_shapes=[
             pltpu.VMEM((cells, c_in), BF16),
             pltpu.VMEM((cells, c_out), BF16),
             pltpu.VMEM((cells, 2 * width), BF16),
             pltpu.VMEM((cells, width), F32),
-            pltpu.VMEM((nodes, cells), BF16),
-            pltpu.VMEM((cells, nodes), BF16),
-            pltpu.VMEM((nodes, ID_ROWS), F32),
             pltpu.VMEM((cells, width), BF16),
+            *[pltpu.VMEM(o.shape, F32) for o in outs],
+            pltpu.SemaphoreType.DMA((5,)),
         ],
-    )(near, far, *weights, *others)
+    )(*map(held, (near, far, *tables, *weights, *others)))
 
 
 def padded(array, sides, width):

time: 32.5 us -> 26.5 us (0.82)
  local copies, waits for them, and re-layouts: 4.51 us -> 0.05 us
  Pallas kernels: 8.96 us -> 7.36 us
  waiting for transfers between devices: 9.15 us -> 9.99 us
  starting transfers between devices: 8.8 us -> 8.23 us
    unnamed x30 -> x9, local copies, waits for them, and re-layouts: 4.49 us -> 0.03 us
    pallas_call x2 -> x3, Pallas kernels: 8.96 us -> 7.36 us  [the longest x1 5.24 us: replicated(): pl.pallas_call(functools.partial(step_kernel, groups), in_specs=[vmem] *...]
    ppermute x4, waiting for transfers between devices: 1.4 us -> 0.47 us  [replicated(): others = tuple((lax.ppermute(w, 'feat', swap) for w in weights))]
    ppermute x1, waiting for transfers between devices: 3.59 us -> 4.38 us  [replicated(): columns.append(lax.ppermute(column, 'tile', ring))]
    ppermute x3, waiting for transfers between devices: 4.15 us -> 4.73 us  [replicated(): blocks.append(lax.ppermute(payload, 'mesh', ring))]
    ppermute x4, starting transfers between devices: 1.09 us -> 0.64 us  [replicated(): others = tuple((lax.ppermute(w, 'feat', swap) for w in weights))]
    ppermute x1, waiting for transfers between devices: 0.01 us -> 0.41 us  [replicated(): far = lax.ppermute(near, 'feat', swap)]
  transfers between devices with their start and end apart: 9 -> 9, of which waited for: 6 -> 6; matrix products, arithmetic and copies ran while one was open for 3% -> 0% of each run, Pallas kernels for 0% -> 4%
where the time goes in v2:
time: 26.5 us; the launch traced here: 26.4 us
  waiting for transfers between devices  9.99 us (38%)
  starting transfers between devices  8.23 us (31%)
  Pallas kernels  7.36 us (28%)
  between operations  0.71 us (3%)
    ppermute x3, starting transfers between devices, replicated(): blocks.append(lax.ppermute(payload, 'mesh', ring))  6.03 us
    pallas_call x1, Pallas kernels, replicated(): pl.pallas_call(functools.partial(step_kernel, groups), in_specs=[vmem] *...  5.24 us
    ppermute x3, waiting for transfers between devices, replicated(): blocks.append(lax.ppermute(payload, 'mesh', ring))  4.73 us
    ppermute x1, waiting for transfers between devices, replicated(): columns.append(lax.ppermute(column, 'tile', ring))  4.38 us
    ppermute x1, starting transfers between devices, replicated(): columns.append(lax.ppermute(column, 'tile', ring))  1.49 us
    pallas_call x1, Pallas kernels, replicated(): pl.pallas_call(functools.partial(index_kernel, mesh_count, tile_count, de...  1.15 us
    pallas_call x1, Pallas kernels, replicated(): pl.pallas_call(pack_kernel, in_specs=[vmem] * 6, out_specs=vmem, out_shap...  0.97 us
    ppermute x4, starting transfers between devices, replicated(): others = tuple((lax.ppermute(w, 'feat', swap) for w in weights))  0.64 us
  transfers between devices with their start and end apart: 9, of which 6 were waited for; matrix products, arithmetic and copies ran while one was open for 0% of the time, Pallas kernels for 4%

profile of v2, /device:TPU:0, one launch (start us, length us, event | category | flops | bytes accessed | tf_op | source)
XLA Modules:
  0.0 26.4 jit_solution(5236333014587647629)
XLA Ops:
  0.6 0.0 copy-start.2
  0.6 0.0 copy-start.3
  0.7 1.0 %shard_map.137 = bf16[144,128]{1,0:T(8,128)(2,1)S(1)} custom-call(bf16[128,128]{1,0:T(8,128)(2,1)} %fields.1, s32[1,128]{1,0:T(1,128)} %bitcast.5, s32[1,128]{1,0:T(1,128)} %bitcast.6, s32[8,32]{1,0:T(8,128)} %bitcast.4, s32[1,32]{1,0:T(1,128)} %bitcast.7, f32[128,128]{1,0:T(8,128)} %cotangent.1), custom_call_target="tpu_custom_call" | custom-call | tf_op jit(solution)/shard_map/pallas_call | solution.py:264
  1.6 0.6 %collective-permute-start.4 = (bf16[512,256]{1,0:T(8,128)(2,1)}, bf16[512,256]{1,0:T(8,128)(2,1)S(1)}, u32[]{:S(2)}, u32[]{:S(2)}) collective-permute-start(bf16[512,256]{1,0:T(8,128)(2,1)} %wp_own), channel_id=1, source_target_pairs={{0,1},{1,0},{2,3},{3,2},{4,5},{5,4},{6,7},{7,6},{8,9},{9,8},{10,11... | collective-permute-start | bytes 786440 | tf_op jit(solution)/shard_map/ppermute | solution.py:283
  2.2 0.1 collective-permute-start.5
  2.3 5.0 %collective-permute-start.2 = (bf16[144,128]{1,0:T(8,128)(2,1)S(1)}, bf16[144,128]{1,0:T(8,128)(2,1)S(1)}, u32[]{:S(2)}, u32[]{:S(2)}) collective-permute-start(bf16[144,128]{1,0:T(8,128)(2,1)S(1)} %shard_map.137), channel_id=1, source_target_pairs={{0,12},{4,0},{8,4},{12,8},{1,13},{5,1},{9,5},{13,9},{2,14},{6,2},{... | collective-permute-start | bytes 110600 | tf_op jit(solution)/shard_map/ppermute | solution.py:282
  7.3 0.0 collective-permute-start.1
  7.3 1.0 %collective-permute-start = (bf16[144,128]{1,0:T(8,128)(2,1)S(1)}, bf16[144,128]{1,0:T(8,128)(2,1)S(1)}, u32[]{:S(2)}, u32[]{:S(2)}) collective-permute-start(bf16[144,128]{1,0:T(8,128)(2,1)S(1)} %shard_map.137), channel_id=1, source_target_pairs={{0,4},{4,8},{8,12},{12,0},{1,5},{5,9},{9,13},{13,1},{2,6},{6,10},{... | collective-permute-start | bytes 110600 | tf_op jit(solution)/shard_map/ppermute | solution.py:282
  8.3 0.8 %collective-permute-done.2 = bf16[144,128]{1,0:T(8,128)(2,1)S(1)} collective-permute-done((bf16[144,128]{1,0:T(8,128)(2,1)S(1)}, bf16[144,128]{1,0:T(8,128)(2,1)S(1)}, u32[]{:S(2)}, u32[]{:S(2)}) %collective-permute-start.2) | collective-permute-done | bytes 36896 | tf_op jit(solution)/shard_map/ppermute | solution.py:282
  9.1 0.0 copy-done.2
  9.1 0.0 collective-permute-start.3
  9.1 3.2 %collective-permute-done.1 = bf16[144,128]{1,0:T(8,128)(2,1)S(1)} collective-permute-done((bf16[144,128]{1,0:T(8,128)(2,1)S(1)}, bf16[144,128]{1,0:T(8,128)(2,1)S(1)}, u32[]{:S(2)}, u32[]{:S(2)}) %collective-permute-start.1) | collective-permute-done | bytes 36896 | tf_op jit(solution)/shard_map/ppermute | solution.py:282
  12.3 0.0 copy-done.3
  12.3 0.0 collective-permute-start.6
  12.3 0.8 %collective-permute-done = bf16[144,128]{1,0:T(8,128)(2,1)S(1)} collective-permute-done((bf16[144,128]{1,0:T(8,128)(2,1)S(1)}, bf16[144,128]{1,0:T(8,128)(2,1)S(1)}, u32[]{:S(2)}, u32[]{:S(2)}) %collective-permute-start) | collective-permute-done | bytes 36896 | tf_op jit(solution)/shard_map/ppermute | solution.py:282
  13.1 0.0 collective-permute-done.3.we_oth
  13.1 0.5 %collective-permute-done.6.wd_oth = bf16[256,128]{1,0:T(8,128)(2,1)S(1)} collective-permute-done((bf16[256,128]{1,0:T(8,128)(2,1)S(1)}, bf16[256,128]{1,0:T(8,128)(2,1)S(1)}, u32[]{:S(2)}, u32[]{:S(2)}) %collective-permute-start.6) | collective-permute-done | bytes 65568 | tf_op jit(solution)/shard_map/ppermute | solution.py:283
  13.5 0.0 collective-permute-done.4.wp_oth
  13.5 0.0 collective-permute-done.5.wc_oth
  13.5 1.5 %collective-permute-start.7 = (bf16[576,128]{1,0:T(8,128)(2,1)S(1)}, bf16[576,128]{1,0:T(8,128)(2,1)S(1)}, u32[]{:S(2)}, u32[]{:S(2)}) collective-permute-start(bf16[576,128]{1,0:T(8,128)(2,1)S(1)} %pad_maximum_fusion), channel_id=1, source_target_pairs={{0,2},{2,0},{1,3},{3,1},{4,6},{6,4},{5,7},{7,5},{8,10},{10,8},{9,1... | collective-permute-start | bytes 442376 | tf_op jit(solution)/shard_map/ppermute | solution.py:289
  15.0 0.0 copy-start
  15.0 0.0 copy-start.1
  15.1 4.4 %collective-permute-done.7 = bf16[576,128]{1,0:T(8,128)(2,1)S(1)} collective-permute-done((bf16[576,128]{1,0:T(8,128)(2,1)S(1)}, bf16[576,128]{1,0:T(8,128)(2,1)S(1)}, u32[]{:S(2)}, u32[]{:S(2)}) %collective-permute-start.7) | collective-permute-done | bytes 147488 | tf_op jit(solution)/shard_map/ppermute | solution.py:289
  19.5 0.1 collective-permute-start.8
  19.5 1.2 %shard_map.138 = (bf16[256,1024]{1,0:T(8,128)(2,1)S(1)}, bf16[1024,256]{1,0:T(8,128)(2,1)S(1)}, bf16[256,256]{1,0:T(8,128)(2,1)S(1)}, bf16[256,16]{1,0:T(8,128)(2,1)S(1)}) custom-call(bf16[1152,128]{1,0:T(8,128)(2,1)S(1)} %constant_dynamic-update-slice_fusion.near), custom_call_target="tpu_custom_call" | custom-call | tf_op jit(solution)/shard_map/pallas_call | solution.py:294
  20.7 0.4 %collective-permute-done.8.far = bf16[1152,128]{1,0:T(8,128)(2,1)S(1)} collective-permute-done((bf16[1152,128]{1,0:T(8,128)(2,1)S(1)}, bf16[1152,128]{1,0:T(8,128)(2,1)S(1)}, u32[]{:S(2)}, u32[]{:S(2)}) %collective-permute-start.8) | collective-permute-done | bytes 294944 | tf_op jit(solution)/shard_map/ppermute | solution.py:291
  21.1 0.0 copy-done
  21.1 0.0 copy-done.1
  21.1 5.2 %shard_map.139 = (f32[128,128]{1,0:T(8,128)}, f32[128,256]{1,0:T(8,128)}, f32[512,256]{1,0:T(8,128)}, f32[512,256]{1,0:T(8,128)}, f32[256,128]{1,0:T(8,128)}) custom-call(bf16[1152,128]{1,0:T(8,128)(2,1)S(1)} %constant_dynamic-update-slice_fusion.near, bf16[1152,128]{1,0:T(8,128)(2,1)S(1)} %collective-permute-done.8.far, ...), custom_call_target="tpu_custom_call" | custom-call | tf_op jit(solution)/shard_map/pallas_call | solution.py:313
  (3 shorter events, 0.0 us)
Async XLA Ops:
  0.6 8.4 %copy-start.2 = (bf16[128,256]{1,0:T(8,128)(2,1)S(1)}, bf16[128,256]{1,0:T(8,128)(2,1)}, u32[]{:S(2)}) copy-start(bf16[128,256]{1,0:T(8,128)(2,1)} %we_own) | copy-start | bytes 196612
  0.6 11.6 %copy-start.3 = (bf16[256,128]{1,0:T(8,128)(2,1)S(1)}, bf16[256,128]{1,0:T(8,128)(2,1)}, u32[]{:S(2)}) copy-start(bf16[256,128]{1,0:T(8,128)(2,1)} %wd_own) | copy-start | bytes 196612
  1.6 11.9 %collective-permute-start.4 = (bf16[512,256]{1,0:T(8,128)(2,1)}, bf16[512,256]{1,0:T(8,128)(2,1)S(1)}, u32[]{:S(2)}, u32[]{:S(2)}) collective-permute-start(bf16[512,256]{1,0:T(8,128)(2,1)} %wp_own), channel_id=1, source_target_pairs={{0,1},{1,0},{2,3},{3,2},{4,5},{5,4},{6,7},{7,6},{8,9},{9,8},{10,11... | collective-permute-start | bytes 786440 | tf_op jit(solution)/shard_map/ppermute | solution.py:283
  2.2 11.3 %collective-permute-start.5 = (bf16[512,256]{1,0:T(8,128)(2,1)}, bf16[512,256]{1,0:T(8,128)(2,1)S(1)}, u32[]{:S(2)}, u32[]{:S(2)}) collective-permute-start(bf16[512,256]{1,0:T(8,128)(2,1)} %wc_own), channel_id=1, source_target_pairs={{0,1},{1,0},{2,3},{3,2},{4,5},{5,4},{6,7},{7,6},{8,9},{9,8},{10,11... | collective-permute-start | bytes 786440 | tf_op jit(solution)/shard_map/ppermute | solution.py:283
  2.3 6.8 %collective-permute-start.2 = (bf16[144,128]{1,0:T(8,128)(2,1)S(1)}, bf16[144,128]{1,0:T(8,128)(2,1)S(1)}, u32[]{:S(2)}, u32[]{:S(2)}) collective-permute-start(bf16[144,128]{1,0:T(8,128)(2,1)S(1)} %shard_map.137), channel_id=1, source_target_pairs={{0,12},{4,0},{8,4},{12,8},{1,13},{5,1},{9,5},{13,9},{2,14},{6,2},{... | collective-permute-start | bytes 110600 | tf_op jit(solution)/shard_map/ppermute | solution.py:282
  7.3 5.0 %collective-permute-start.1 = (bf16[144,128]{1,0:T(8,128)(2,1)S(1)}, bf16[144,128]{1,0:T(8,128)(2,1)S(1)}, u32[]{:S(2)}, u32[]{:S(2)}) collective-permute-start(bf16[144,128]{1,0:T(8,128)(2,1)S(1)} %shard_map.137), channel_id=1, source_target_pairs={{0,8},{4,12},{8,0},{12,4},{1,9},{5,13},{9,1},{13,5},{2,10},{6,14},... | collective-permute-start | bytes 110600 | tf_op jit(solution)/shard_map/ppermute | solution.py:282
  7.3 5.8 %collective-permute-start = (bf16[144,128]{1,0:T(8,128)(2,1)S(1)}, bf16[144,128]{1,0:T(8,128)(2,1)S(1)}, u32[]{:S(2)}, u32[]{:S(2)}) collective-permute-start(bf16[144,128]{1,0:T(8,128)(2,1)S(1)} %shard_map.137), channel_id=1, source_target_pairs={{0,4},{4,8},{8,12},{12,0},{1,5},{5,9},{9,13},{13,1},{2,6},{6,10},{... | collective-permute-start | bytes 110600 | tf_op jit(solution)/shard_map/ppermute | solution.py:282
  9.1 4.0 %collective-permute-start.3 = (bf16[128,256]{1,0:T(8,128)(2,1)S(1)}, bf16[128,256]{1,0:T(8,128)(2,1)S(1)}, u32[]{:S(2)}, u32[]{:S(2)}) collective-permute-start(bf16[128,256]{1,0:T(8,128)(2,1)S(1)} %copy-done.2), channel_id=1, source_target_pairs={{0,1},{1,0},{2,3},{3,2},{4,5},{5,4},{6,7},{7,6},{8,9},{9,8},{10,11... | collective-permute-start | bytes 196616 | tf_op jit(solution)/shard_map/ppermute | solution.py:283
  12.3 1.3 %collective-permute-start.6 = (bf16[256,128]{1,0:T(8,128)(2,1)S(1)}, bf16[256,128]{1,0:T(8,128)(2,1)S(1)}, u32[]{:S(2)}, u32[]{:S(2)}) collective-permute-start(bf16[256,128]{1,0:T(8,128)(2,1)S(1)} %copy-done.3), channel_id=1, source_target_pairs={{0,1},{1,0},{2,3},{3,2},{4,5},{5,4},{6,7},{7,6},{8,9},{9,8},{10,11... | collective-permute-start | bytes 196616 | tf_op jit(solution)/shard_map/ppermute | solution.py:283
  13.5 5.9 %collective-permute-start.7 = (bf16[576,128]{1,0:T(8,128)(2,1)S(1)}, bf16[576,128]{1,0:T(8,128)(2,1)S(1)}, u32[]{:S(2)}, u32[]{:S(2)}) collective-permute-start(bf16[576,128]{1,0:T(8,128)(2,1)S(1)} %pad_maximum_fusion), channel_id=1, source_target_pairs={{0,2},{2,0},{1,3},{3,1},{4,6},{6,4},{5,7},{7,5},{8,10},{10,8},{9,1... | collective-permute-start | bytes 442376 | tf_op jit(solution)/shard_map/ppermute | solution.py:289
  15.0 6.1 %copy-start = (bf16[512,256]{1,0:T(8,128)(2,1)S(1)}, bf16[512,256]{1,0:T(8,128)(2,1)}, u32[]{:S(2)}) copy-start(bf16[512,256]{1,0:T(8,128)(2,1)} %wp_own) | copy-start | bytes 786436
  15.0 6.1 %copy-start.1 = (bf16[512,256]{1,0:T(8,128)(2,1)S(1)}, bf16[512,256]{1,0:T(8,128)(2,1)}, u32[]{:S(2)}) copy-start(bf16[512,256]{1,0:T(8,128)(2,1)} %wc_own) | copy-start | bytes 786436
  19.5 1.6 %collective-permute-start.8 = (bf16[1152,128]{1,0:T(8,128)(2,1)S(1)}, bf16[1152,128]{1,0:T(8,128)(2,1)S(1)}, u32[]{:S(2)}, u32[]{:S(2)}) collective-permute-start(bf16[1152,128]{1,0:T(8,128)(2,1)S(1)} %constant_dynamic-update-slice_fusion.near), channel_id=1, source_target_pairs={{0,1},{1,0},{2,3},{3,2},{4,5},{5,4},{6,7},{7,6},{8,9},{9,8},{10,11... | collective-permute-start | bytes 884744 | tf_op jit(solution)/shard_map/ppermute | solution.py:291

commit v3 on v2

--- a/solution.py
+++ b/solution.py
@@ -7,10 +7,12 @@
 from jax.experimental.pallas import tpu as pltpu
 from jax.sharding import PartitionSpec as P
 
+
 MA = 4
 MB = 8
 CPD = 2
 ID_ROWS = 16
+GRANT = 20 << 20
 REPLICATE_LIMIT = 1 << 20
 
 F32 = jnp.float32
@@ -54,26 +56,84 @@
     out[rows : rows + ID_ROWS, :] = wide[...].astype(BF16)
 
 
-def index_kernel(mesh_count, tile_count, degree, near, hit, hit_t, reach_out, member_out, ids):
+def tags_at(ref, start):
+    tags = ref[pl.ds(start, ID_ROWS), :].astype(F32)
+    return tags, jnp.transpose(tags)
+
+
+def hits(tags, tags_t, nodes):
+    local = MA * MB
+    rows = tags.shape[1]
+    sub = lax.broadcasted_iota(jnp.int32, (nodes, rows), 0).astype(F32)
+    lane = lax.broadcasted_iota(jnp.int32, (rows, nodes), 1).astype(F32)
+    by_node = (sub == tags[0:1, :] * local + tags[1:2, :]).astype(BF16)
+    by_cell = (lane == tags_t[:, 0:1] * local + tags_t[:, 1:2]).astype(BF16)
+    return by_node, by_cell
+
+
+def near_kernel(
+    groups,
+    near,
+    far,
+    we_own,
+    we_oth,
+    node_part,
+    cot_part,
+    dec_part,
+    hid_own,
+    slope,
+    hit_t,
+    cells,
+    cots,
+    hit,
+    hid,
+):
+    nodes = groups * MA * MB
+    rows, width = hid_own.shape[0], we_own.shape[1]
+    block = rows + ID_ROWS
+    core = lax.axis_index("feat")
+    for p in range(near.shape[0] // block):
+        span = slice(p * rows, (p + 1) * rows)
+        here = pl.ds(p * block, rows)
+        hit[:, span], hit_t[span, :] = hits(*tags_at(near, p * block + rows), nodes)
+        a, b = near[here, :], far[here, :]
+        cell = jnp.where(core == 0, a, b)
+        cells[span, :] = cell
+        cots[span, :] = jnp.where(core == 0, b, a)
+        pre = mm(cell, we_own[...])
+        sig = jax.nn.sigmoid(pre)
+        act = pre * sig
+        hid[span, 0:width] = act.astype(BF16)
+        slope[span, :] = sig + act * (1.0 - sig)
+        pre = mm(cell, we_oth[...])
+        hid[span, width:] = (pre * jax.nn.sigmoid(pre)).astype(BF16)
+    cot = cots[...]
+    hid_own[...] = hid[0:rows, :]
+    node_part[...] = mm(hit[...], hid[...])
+    cot_part[...] = mm(hit[...], cot)
+    dec_part[...] = mm(hid[:, :width], cot, TN)
+
+
+def index_kernel(
+    mesh_count, tile_count, degree, near, rest, hit, reach_out, member_out, ids
+):
     groups = mesh_count * tile_count
     local = MA * MB
     nodes = groups * local
-    block = near.shape[0] // groups
+    block = near.shape[0] // tile_count
     rows = block - ID_ROWS
     my_mesh = lax.axis_index("mesh")
     my_tile = lax.axis_index("tile")
-    sub = lax.broadcasted_iota(jnp.int32, (nodes, rows), 0).astype(F32)
-    lane = lax.broadcasted_iota(jnp.int32, (rows, nodes), 1).astype(F32)
     for p in range(groups):
-        far_tile, shift = p // mesh_count, p % mesh_count
+        shift, turn = p // tile_count, p % tile_count
         group = lax.rem(my_mesh - shift + mesh_count, mesh_count) * tile_count + lax.rem(
-            my_tile - far_tile + tile_count, tile_count
+            my_tile - turn + tile_count, tile_count
         )
-        span = slice(p * rows, (p + 1) * rows)
-        tags = near[pl.ds(p * block + rows, ID_ROWS), :].astype(F32)
-        tags_t = jnp.transpose(tags)
-        hit[:, span] = (sub == tags[0:1, :] * local + tags[1:2, :]).astype(BF16)
-        hit_t[span, :] = (lane == tags_t[:, 0:1] * local + tags_t[:, 1:2]).astype(BF16)
+        q = p - tile_count
+        tags, tags_t = tags_at(near, p * block + rows) if q < 0 else tags_at(rest, q * block + rows)
+        if q >= 0:
+            span = slice(q * rows, (q + 1) * rows)
+            hit[:, span] = hits(tags, tags_t, nodes)[0]
         ids[pl.ds(pl.multiple_of(group * local, local), local), :] = tags_t[0:local, :]
 
     tags = ids[...].astype(jnp.int32)
@@ -98,11 +158,18 @@
 
 
 def step_kernel(
-    groups,
-    near,
+    near_count,
+    rest,
     far,
+    node_part,
+    cot_part,
+    dec_part,
+    hid_own,
+    slope_near,
+    hit_t_near,
+    cells_near,
+    cots_near,
     hit,
-    hit_t,
     reach_ref,
     member_ref,
     we_own,
@@ -123,6 +190,8 @@
     hid,
     slope,
     gpe,
+    gpe_near,
+    hit_t,
     prediction,
     encode_grad,
     process_grad,
@@ -130,9 +199,9 @@
     decode_grad,
     sems,
 ):
-    block = near.shape[0] // groups
-    rows = block - ID_ROWS
-    width = we_own.shape[1]
+    rows, width = hid_own.shape[0], we_own.shape[1]
+    block = rows + ID_ROWS
+    count = rest.shape[0] // block
     core = lax.axis_index("feat")
     own = pl.ds(pl.multiple_of(core * width, width), width)
     oth = pl.ds(pl.multiple_of((1 - core) * width, width), width)
@@ -148,10 +217,11 @@
             )
         )
     ]
-    for p in range(groups):
+    nodes = hit.shape[0]
+    for p in range(count):
         here = pl.ds(p * block, rows)
         span = slice(p * rows, (p + 1) * rows)
-        a, b = near[here, :], far[here, :]
+        a, b = rest[here, :], far[here, :]
         cell = jnp.where(core == 0, a, b)
         cells[span, :] = cell
         cots[span, :] = jnp.where(core == 0, b, a)
@@ -162,10 +232,11 @@
         slope[span, :] = sig + act * (1.0 - sig)
         pre = mm(cell, we_oth[...])
         hid[span, width:] = (pre * jax.nn.sigmoid(pre)).astype(BF16)
+        hit_t[span, :] = hits(*tags_at(rest, p * block + rows), nodes)[1]
 
     reach = reach_ref[...]
     member = member_ref[...]
-    node_in = mm(hit[...], hid[...]).astype(BF16)
+    node_in = (node_part[...] + mm(hit[...], hid[...])).astype(BF16)
     agg = mm(reach, node_in).astype(BF16)
     agg_own, agg_oth = agg[:, :width], agg[:, width:]
     pre_mesh = (
@@ -191,29 +262,33 @@
     level_two = tuple(
         (v + mm(member, c.astype(BF16))).astype(BF16) for v, c in zip(level_one, act_coarse)
     )
-    mine = hit_t[0:rows, :]
+    mine = hit_t_near[0:rows, :]
     merged = (
-        (hid[0:rows, :width].astype(F32) + mm(mine, level_two[0])).astype(BF16),
-        (hid[0:rows, width:].astype(F32) + mm(mine, level_two[1])).astype(BF16),
+        (hid_own[:, :width].astype(F32) + mm(mine, level_two[0])).astype(BF16),
+        (hid_own[:, width:].astype(F32) + mm(mine, level_two[1])).astype(BF16),
     )
     prediction[...] = mm(merged[0], wd_own[...]) + mm(merged[1], wd_oth[...])
-    sent[0].start()
 
     cot = cots[...]
-    node_cot = mm(hit[...], cot)
+    node_cot = cot_part[...] + mm(hit[...], cot)
     cot_high, cot_low = split(node_cot)
-    decode_grad[...] = mm(hid[:, :width], cot, TN) + mm(level_two[0], cot_high, TN)
-    sent[4].start()
+    decode_grad[...] = (
+        dec_part[...] + mm(hid[:, :width], cot, TN) + mm(level_two[0], cot_high, TN)
+    )
     grad_two = tuple(mm(cot_high, w[...], NT) + mm(cot_low, w[...], NT) for w in (wd_own, wd_oth))
-    grad_pre_coarse = []
+    gpc = []
     for g, s, c in zip(grad_two, sig_coarse, act_coarse):
         high, low = split(g)
         total = mm(member, high, TN) + mm(member, low, TN)
-        grad_pre_coarse.append(total * (s + c * (1.0 - s)))
-    gpc = [v.astype(BF16) for v in grad_pre_coarse]
+        gpc.append((total * (s + c * (1.0 - s))).astype(BF16))
     coarse_grad[own, :] = mm(coarse_in[0], gpc[0], TN)
     coarse_grad[oth, :] = mm(coarse_in[1], gpc[0], TN)
-    sent[3].start()
+
+    @pl.when(core >= 0)
+    def _():
+        for i in (0, 3, 4):
+            sent[i].start()
+
     grad_coarse_in = (
         mm(gpc[0], wc_own[own, :], NT) + mm(gpc[1], wc_oth[own, :], NT),
         mm(gpc[0], wc_own[oth, :], NT) + mm(gpc[1], wc_oth[oth, :], NT),
@@ -224,14 +299,22 @@
     )
     process_grad[own, :] = mm(agg_own, gpm[0], TN)
     process_grad[oth, :] = mm(agg_oth, gpm[0], TN)
-    sent[2].start()
+
+    @pl.when(core >= 0)
+    def _():
+        sent[2].start()
+
     grad_agg = (mm(gpm[0], wp_own[own, :], NT) + mm(gpm[1], wp_oth[own, :], NT)).astype(BF16)
     grad_zero = (grad_one[0] + mm(reach, grad_agg, TN)).astype(BF16)
-    for p in range(groups):
+    for p in range(count):
         span = slice(p * rows, (p + 1) * rows)
         grad_hidden = mm(cots[span, :], wd_own[...], NT) + mm(hit_t[span, :], grad_zero)
         gpe[span, :] = (grad_hidden * slope[span, :]).astype(BF16)
-    encode_grad[...] = mm(cells[...], gpe[...], TN)
+    for p in range(near_count):
+        span = slice(p * rows, (p + 1) * rows)
+        grad_hidden = mm(cots_near[span, :], wd_own[...], NT) + mm(hit_t_near[span, :], grad_zero)
+        gpe_near[span, :] = (grad_hidden * slope_near[span, :]).astype(BF16)
+    encode_grad[...] = mm(cells[...], gpe[...], TN) + mm(cells_near[...], gpe_near[...], TN)
     sent[1].start()
     for copy in sent:
         copy.wait()
@@ -261,6 +344,7 @@
     swap = [(0, 1), (1, 0)]
     vmem = pl.BlockSpec(memory_space=pltpu.VMEM)
     hbm = pl.BlockSpec(memory_space=pl.ANY)
+    grant = pltpu.CompilerParams(vmem_limit_bytes=GRANT)
     payload = pl.pallas_call(
         pack_kernel,
         in_specs=[vmem] * 6,
@@ -275,34 +359,56 @@
         coarse_ids.reshape(1, MA * MB),
         cotangent,
     )
-    payload, weights = lax.optimization_barrier((payload, weights))
-    blocks = [payload]
+    columns = [payload]
+    for turn in range(1, tile_count):
+        ring = [(i, (i + turn) % tile_count) for i in range(tile_count)]
+        columns.append(lax.ppermute(payload, "tile", ring))
+    near = jnp.concatenate(columns, axis=0)
+    near, weights = lax.optimization_barrier((near, weights))
+    blocks = []
     for shift in range(1, mesh_count):
         ring = [(i, (i + shift) % mesh_count) for i in range(mesh_count)]
-        blocks.append(lax.ppermute(payload, "mesh", ring))
+        blocks.append(lax.ppermute(near, "mesh", ring))
+    near_far = lax.ppermute(near, "feat", swap)
     others = tuple(lax.ppermute(w, "feat", swap) for w in weights)
-    column = jnp.concatenate(blocks, axis=0)
-    column, others = lax.optimization_barrier((column, others))
-    columns = [column]
-    for shift in range(1, tile_count):
-        ring = [(i, (i + shift) % tile_count) for i in range(tile_count)]
-        columns.append(lax.ppermute(column, "tile", ring))
-    near = jnp.concatenate(columns, axis=0)
-    far = lax.ppermute(near, "feat", swap)
-    cells = groups * rows
     degree = stencil_codes.shape[1]
+    beside = tile_count * rows
+    near_call = pl.pallas_call(
+        functools.partial(near_kernel, groups),
+        in_specs=[vmem] * 4,
+        compiler_params=grant,
+        out_specs=[vmem] * 8,
+        out_shape=(
+            pltpu.VMEM((nodes, 2 * width), F32),
+            pltpu.VMEM((nodes, c_out), F32),
+            pltpu.VMEM((width, c_out), F32),
+            pltpu.VMEM((rows, 2 * width), BF16),
+            pltpu.VMEM((beside, width), F32),
+            pltpu.VMEM((beside, nodes), BF16),
+            pltpu.VMEM((beside, c_in), BF16),
+            pltpu.VMEM((beside, c_out), BF16),
+        ),
+        scratch_shapes=[
+            pltpu.VMEM((nodes, beside), BF16),
+            pltpu.VMEM((beside, 2 * width), BF16),
+        ],
+    )
+    parts = near_call(*map(held, (near, near_far, encode_weight, others[0])))
+    rest = jnp.concatenate(blocks, axis=0)
+    rest_far = lax.ppermute(rest, "feat", swap)
+    cells = (groups - tile_count) * rows
     tables = pl.pallas_call(
         functools.partial(index_kernel, mesh_count, tile_count, degree),
-        in_specs=[vmem],
-        out_specs=[vmem] * 4,
+        in_specs=[vmem] * 2,
+        compiler_params=grant,
+        out_specs=[vmem] * 3,
         out_shape=(
             pltpu.VMEM((nodes, cells), BF16),
-            pltpu.VMEM((cells, nodes), BF16),
             pltpu.VMEM((nodes, nodes), BF16),
             pltpu.VMEM((nodes, CPD * groups), BF16),
         ),
         scratch_shapes=[pltpu.VMEM((nodes, ID_ROWS), F32)],
-    )(held(near))
+    )(held(near), held(rest))
     outs = (
         jax.ShapeDtypeStruct((rows, c_out), F32),
         jax.ShapeDtypeStruct((c_in, width), F32),
@@ -310,9 +416,11 @@
         jax.ShapeDtypeStruct(coarse_weight.shape, F32),
         jax.ShapeDtypeStruct((width, c_out), F32),
     )
+    operands = [held(v) for v in (rest, rest_far, *parts, *tables, *weights, *others)]
     return pl.pallas_call(
-        functools.partial(step_kernel, groups),
-        in_specs=[vmem] * 14,
+        functools.partial(step_kernel, tile_count),
+        in_specs=[vmem] * len(operands),
+        compiler_params=grant,
         out_specs=[hbm] * 5,
         out_shape=outs,
         scratch_shapes=[
@@ -321,10 +429,12 @@
             pltpu.VMEM((cells, 2 * width), BF16),
             pltpu.VMEM((cells, width), F32),
             pltpu.VMEM((cells, width), BF16),
+            pltpu.VMEM((beside, width), BF16),
+            pltpu.VMEM((cells, nodes), BF16),
             *[pltpu.VMEM(o.shape, F32) for o in outs],
             pltpu.SemaphoreType.DMA((5,)),
         ],
-    )(*map(held, (near, far, *tables, *weights, *others)))
+    )(*operands)
 
 
 def padded(array, sides, width):
@@ -527,7 +637,8 @@
     cells, nodes = groups * rows, groups * MA * MB
     degree = stencil_codes.shape[1]
     fits = (
-        cells * nodes <= REPLICATE_LIMIT
+        groups > lax.axis_size("tile")
+        and cells * nodes <= REPLICATE_LIMIT
         and lax.axis_size("feat") == 2
         and rows == c_in == rest[-1].shape[1]
         and max(nodes, 25) <= 256

time: 26.5 us -> 26.3 us (level)
  waiting for transfers between devices: 9.99 us -> 7.65 us
  starting transfers between devices: 8.23 us -> 9.42 us
  local copies, waits for them, and re-layouts: 0.05 us -> 0.75 us
    ppermute x5 -> x6, waiting for transfers between devices: 9.52 us -> 6.9 us  [the longest x3 4.96 us: replicated(): blocks.append(lax.ppermute(near, 'mesh', ring))]
    ppermute x5 -> x6, starting transfers between devices: 7.59 us -> 8.75 us  [the longest x3 5.14 us: replicated(): blocks.append(lax.ppermute(near, 'mesh', ring))]
    unnamed x9 -> x10, local copies, waits for them, and re-layouts: 0.03 us -> 0.74 us
    pallas_call x1 -> x2, Pallas kernels: 5.24 us -> 5.75 us  [the longest x1 5.19 us: replicated(): pl.pallas_call(functools.partial(step_kernel, tile_count), in_specs=[vmem...]
    pallas_call x1, Pallas kernels: 1.15 us -> 0.81 us  [replicated(): pl.pallas_call(functools.partial(index_kernel, mesh_count, tile_count, de...]
    ppermute x4, waiting for transfers between devices: 0.47 us -> 0.75 us  [replicated(): others = tuple((lax.ppermute(w, 'feat', swap) for w in weights))]
  transfers between devices with their start and end apart: 9 -> 10, of which waited for: 6 -> 4; matrix products, arithmetic and copies ran while one was open for 0% -> 0% of each run, Pallas kernels for 4% -> 5%
where the time goes in v3:
time: 26.3 us; the launch traced here: 26.1 us
  starting transfers between devices  9.42 us (36%)
  waiting for transfers between devices  7.65 us (29%)
  Pallas kernels  7.53 us (29%)
  between operations  0.76 us (3%)
  local copies, waits for them, and re-layouts  0.75 us (3%)
    pallas_call x1, Pallas kernels, replicated(): pl.pallas_call(functools.partial(step_kernel, tile_count), in_specs=[vmem...  5.19 us
    ppermute x3, starting transfers between devices, replicated(): blocks.append(lax.ppermute(near, 'mesh', ring))  5.14 us
    ppermute x3, waiting for transfers between devices, replicated(): blocks.append(lax.ppermute(near, 'mesh', ring))  4.96 us
    ppermute x1, starting transfers between devices, replicated(): columns.append(lax.ppermute(payload, 'tile', ring))  3.03 us
    ppermute x1, waiting for transfers between devices, replicated(): columns.append(lax.ppermute(payload, 'tile', ring))  1.94 us
    pallas_call x1, Pallas kernels, replicated(): pl.pallas_call(pack_kernel, in_specs=[vmem] * 6, out_specs=vmem, out_shap...  0.98 us
    pallas_call x1, Pallas kernels, replicated(): pl.pallas_call(functools.partial(index_kernel, mesh_count, tile_count, de...  0.81 us
    ppermute x4, waiting for transfers between devices, replicated(): others = tuple((lax.ppermute(w, 'feat', swap) for w in weights))  0.75 us
  transfers between devices with their start and end apart: 10, of which 4 were waited for; matrix products, arithmetic and copies ran while one was open for 0% of the time, Pallas kernels for 5%

profile of v3, /device:TPU:0, one launch (start us, length us, event | category | flops | bytes accessed | tf_op | source)
XLA Modules:
  0.0 26.1 jit_solution(12076672253061850541)
XLA Ops:
  0.6 0.0 copy-start
  0.6 1.0 %shard_map.137 = bf16[144,128]{1,0:T(8,128)(2,1)S(1)} custom-call(bf16[128,128]{1,0:T(8,128)(2,1)} %fields.1, s32[1,128]{1,0:T(1,128)} %bitcast.5, s32[1,128]{1,0:T(1,128)} %bitcast.6, s32[8,32]{1,0:T(8,128)} %bitcast.4, s32[1,32]{1,0:T(1,128)} %bitcast.7, f32[128,128]{1,0:T(8,128)} %cotangent.1), custom_call_target="tpu_custom_call" | custom-call | tf_op jit(solution)/shard_map/pallas_call | solution.py:348
  1.6 3.0 %collective-permute-start = (bf16[144,128]{1,0:T(8,128)(2,1)S(1)}, bf16[144,128]{1,0:T(8,128)(2,1)S(1)}, u32[]{:S(2)}, u32[]{:S(2)}) collective-permute-start(bf16[144,128]{1,0:T(8,128)(2,1)S(1)} %shard_map.137), channel_id=1, source_target_pairs={{0,2},{2,0},{1,3},{3,1},{4,6},{6,4},{5,7},{7,5},{8,10},{10,8},{9,1... | collective-permute-start | bytes 110600 | tf_op jit(solution)/shard_map/ppermute | solution.py:365
  4.7 1.9 %collective-permute-done = bf16[144,128]{1,0:T(8,128)(2,1)S(1)} collective-permute-done((bf16[144,128]{1,0:T(8,128)(2,1)S(1)}, bf16[144,128]{1,0:T(8,128)(2,1)S(1)}, u32[]{:S(2)}, u32[]{:S(2)}) %collective-permute-start) | collective-permute-done | bytes 36896 | tf_op jit(solution)/shard_map/ppermute | solution.py:365
  6.6 2.1 %collective-permute-start.1 = (bf16[288,128]{1,0:T(8,128)(2,1)S(1)}, bf16[288,128]{1,0:T(8,128)(2,1)S(1)}, u32[]{:S(2)}, u32[]{:S(2)}) collective-permute-start(bf16[288,128]{1,0:T(8,128)(2,1)S(1)} %pad_maximum_fusion.near), channel_id=1, source_target_pairs={{0,4},{4,8},{8,12},{12,0},{1,5},{5,9},{9,13},{13,1},{2,6},{6,10},{... | collective-permute-start | bytes 221192 | tf_op jit(solution)/shard_map/ppermute | solution.py:371
  8.7 2.1 %collective-permute-start.3 = (bf16[288,128]{1,0:T(8,128)(2,1)S(1)}, bf16[288,128]{1,0:T(8,128)(2,1)S(1)}, u32[]{:S(2)}, u32[]{:S(2)}) collective-permute-start(bf16[288,128]{1,0:T(8,128)(2,1)S(1)} %pad_maximum_fusion.near), channel_id=1, source_target_pairs={{0,12},{4,0},{8,4},{12,8},{1,13},{5,1},{9,5},{13,9},{2,14},{6,2},{... | collective-permute-start | bytes 221192 | tf_op jit(solution)/shard_map/ppermute | solution.py:371
  10.8 1.0 %collective-permute-start.2 = (bf16[288,128]{1,0:T(8,128)(2,1)S(1)}, bf16[288,128]{1,0:T(8,128)(2,1)S(1)}, u32[]{:S(2)}, u32[]{:S(2)}) collective-permute-start(bf16[288,128]{1,0:T(8,128)(2,1)S(1)} %pad_maximum_fusion.near), channel_id=1, source_target_pairs={{0,8},{4,12},{8,0},{12,4},{1,9},{5,13},{9,1},{13,5},{2,10},{6,14},... | collective-permute-start | bytes 221192 | tf_op jit(solution)/shard_map/ppermute | solution.py:371
  11.7 0.0 copy-done
  11.7 0.0 collective-permute-start.7
  11.7 0.5 %collective-permute-start.8 = (bf16[512,256]{1,0:T(8,128)(2,1)}, bf16[512,256]{1,0:T(8,128)(2,1)S(1)}, u32[]{:S(2)}, u32[]{:S(2)}) collective-permute-start(bf16[512,256]{1,0:T(8,128)(2,1)} %wc_own), channel_id=1, source_target_pairs={{0,1},{1,0},{2,3},{3,2},{4,5},{5,4},{6,7},{7,6},{8,9},{9,8},{10,11... | collective-permute-start | bytes 786440 | tf_op jit(solution)/shard_map/ppermute | solution.py:373
  12.3 1.7 %collective-permute-done.1 = bf16[288,128]{1,0:T(8,128)(2,1)S(1)} collective-permute-done((bf16[288,128]{1,0:T(8,128)(2,1)S(1)}, bf16[288,128]{1,0:T(8,128)(2,1)S(1)}, u32[]{:S(2)}, u32[]{:S(2)}) %collective-permute-start.1) | collective-permute-done | bytes 73760 | tf_op jit(solution)/shard_map/ppermute | solution.py:371
  14.0 3.3 %collective-permute-done.2 = bf16[288,128]{1,0:T(8,128)(2,1)S(1)} collective-permute-done((bf16[288,128]{1,0:T(8,128)(2,1)S(1)}, bf16[288,128]{1,0:T(8,128)(2,1)S(1)}, u32[]{:S(2)}, u32[]{:S(2)}) %collective-permute-start.2) | collective-permute-done | bytes 73760 | tf_op jit(solution)/shard_map/ppermute | solution.py:371
  17.2 0.0 copy-start.2
  17.2 0.0 copy-start.3
  17.3 0.0 collective-permute-done.3
  17.3 0.0 copy-start.1
  17.3 0.1 collective-permute-start.4
  17.4 0.7 %copy-done.2 = bf16[128,256]{1,0:T(8,128)(2,1)S(1)} copy-done((bf16[128,256]{1,0:T(8,128)(2,1)S(1)}, bf16[128,256]{1,0:T(8,128)(2,1)}, u32[]{:S(2)}) %copy-start.2) | copy-done | bytes 65560
  18.1 0.0 collective-permute-start.6
  18.1 0.5 %collective-permute-start.5 = (bf16[288,128]{1,0:T(8,128)(2,1)S(1)}, bf16[288,128]{1,0:T(8,128)(2,1)S(1)}, u32[]{:S(2)}, u32[]{:S(2)}) collective-permute-start(bf16[288,128]{1,0:T(8,128)(2,1)S(1)} %pad_maximum_fusion.near), channel_id=1, source_target_pairs={{0,1},{1,0},{2,3},{3,2},{4,5},{5,4},{6,7},{7,6},{8,9},{9,8},{10,11... | collective-permute-start | bytes 221192 | tf_op jit(solution)/shard_map/ppermute | solution.py:372
  18.6 0.7 %collective-permute-done.6.we_oth = bf16[128,256]{1,0:T(8,128)(2,1)S(1)} collective-permute-done((bf16[128,256]{1,0:T(8,128)(2,1)S(1)}, bf16[128,256]{1,0:T(8,128)(2,1)S(1)}, u32[]{:S(2)}, u32[]{:S(2)}) %collective-permute-start.6) | collective-permute-done | bytes 65568 | tf_op jit(solution)/shard_map/ppermute | solution.py:373
  19.3 0.0 copy-done.3
  19.3 0.2 collective-permute-start.9
  19.5 0.8 %shard_map.139 = (bf16[256,768]{1,0:T(8,128)(2,1)S(1)}, bf16[256,256]{1,0:T(8,128)(2,1)S(1)}, bf16[256,16]{1,0:T(8,128)(2,1)S(1)}) custom-call(bf16[288,128]{1,0:T(8,128)(2,1)S(1)} %pad_maximum_fusion.near, bf16[864,128]{1,0:T(8,128)(2,1)S(1)} %constant_dynamic-update-slice_fusion.rest), custom_call_target="tpu_custom_call" | custom-call | tf_op jit(solution)/shard_map/pallas_call | solution.py:400
  20.3 0.0 collective-permute-done.5.far
  20.3 0.6 %shard_map.138 = (f32[256,512]{1,0:T(8,128)S(1)}, f32[256,128]{1,0:T(8,128)S(1)}, f32[256,128]{1,0:T(8,128)S(1)}, bf16[128,512]{1,0:T(8,128)(2,1)S(1)}, f32[256,...) custom-call(bf16[288,128]{1,0:T(8,128)(2,1)S(1)} %pad_maximum_fusion, ...), custom_call_target="tpu_custom_call" | custom-call | tf_op jit(solution)/shard_map/pallas_call | solution.py:396
  20.9 0.0 collective-permute-done.9.wd_oth
  20.9 0.0 collective-permute-done.7.wp_oth
  20.9 0.0 collective-permute-done.8.wc_oth
  20.9 0.0 collective-permute-done.4.far
  20.9 0.0 copy-done.1
  20.9 5.2 %shard_map.140 = (f32[128,128]{1,0:T(8,128)}, f32[128,256]{1,0:T(8,128)}, f32[512,256]{1,0:T(8,128)}, f32[512,256]{1,0:T(8,128)}, f32[256,128]{1,0:T(8,128)}) custom-call(bf16[864,128]{1,0:T(8,128)(2,1)S(1)} %constant_dynamic-update-slice_fusion.rest, bf16[864,128]{1,0:T(8,128)(2,1)S(1)} %collective-permute-done.4.far, ...), custom_call_target="tpu_custom_call" | custom-call | tf_op jit(solution)/shard_map/pallas_call | solution.py:420
  (4 shorter events, 0.0 us)
Async XLA Ops:
  0.6 11.1 %copy-start = (bf16[512,256]{1,0:T(8,128)(2,1)S(1)}, bf16[512,256]{1,0:T(8,128)(2,1)}, u32[]{:S(2)}) copy-start(bf16[512,256]{1,0:T(8,128)(2,1)} %wp_own) | copy-start | bytes 786436
  1.6 5.0 %collective-permute-start = (bf16[144,128]{1,0:T(8,128)(2,1)S(1)}, bf16[144,128]{1,0:T(8,128)(2,1)S(1)}, u32[]{:S(2)}, u32[]{:S(2)}) collective-permute-start(bf16[144,128]{1,0:T(8,128)(2,1)S(1)} %shard_map.137), channel_id=1, source_target_pairs={{0,2},{2,0},{1,3},{3,1},{4,6},{6,4},{5,7},{7,5},{8,10},{10,8},{9,1... | collective-permute-start | bytes 110600 | tf_op jit(solution)/shard_map/ppermute | solution.py:365
  6.6 7.4 %collective-permute-start.1 = (bf16[288,128]{1,0:T(8,128)(2,1)S(1)}, bf16[288,128]{1,0:T(8,128)(2,1)S(1)}, u32[]{:S(2)}, u32[]{:S(2)}) collective-permute-start(bf16[288,128]{1,0:T(8,128)(2,1)S(1)} %pad_maximum_fusion.near), channel_id=1, source_target_pairs={{0,4},{4,8},{8,12},{12,0},{1,5},{5,9},{9,13},{13,1},{2,6},{6,10},{... | collective-permute-start | bytes 221192 | tf_op jit(solution)/shard_map/ppermute | solution.py:371
  8.7 8.6 %collective-permute-start.3 = (bf16[288,128]{1,0:T(8,128)(2,1)S(1)}, bf16[288,128]{1,0:T(8,128)(2,1)S(1)}, u32[]{:S(2)}, u32[]{:S(2)}) collective-permute-start(bf16[288,128]{1,0:T(8,128)(2,1)S(1)} %pad_maximum_fusion.near), channel_id=1, source_target_pairs={{0,12},{4,0},{8,4},{12,8},{1,13},{5,1},{9,5},{13,9},{2,14},{6,2},{... | collective-permute-start | bytes 221192 | tf_op jit(solution)/shard_map/ppermute | solution.py:371
  10.8 6.4 %collective-permute-start.2 = (bf16[288,128]{1,0:T(8,128)(2,1)S(1)}, bf16[288,128]{1,0:T(8,128)(2,1)S(1)}, u32[]{:S(2)}, u32[]{:S(2)}) collective-permute-start(bf16[288,128]{1,0:T(8,128)(2,1)S(1)} %pad_maximum_fusion.near), channel_id=1, source_target_pairs={{0,8},{4,12},{8,0},{12,4},{1,9},{5,13},{9,1},{13,5},{2,10},{6,14},... | collective-permute-start | bytes 221192 | tf_op jit(solution)/shard_map/ppermute | solution.py:371
  11.7 9.2 %collective-permute-start.7 = (bf16[512,256]{1,0:T(8,128)(2,1)S(1)}, bf16[512,256]{1,0:T(8,128)(2,1)S(1)}, u32[]{:S(2)}, u32[]{:S(2)}) collective-permute-start(bf16[512,256]{1,0:T(8,128)(2,1)S(1)} %copy-done), channel_id=1, source_target_pairs={{0,1},{1,0},{2,3},{3,2},{4,5},{5,4},{6,7},{7,6},{8,9},{9,8},{10,11... | collective-permute-start | bytes 786440 | tf_op jit(solution)/shard_map/ppermute | solution.py:373
  11.7 9.2 %collective-permute-start.8 = (bf16[512,256]{1,0:T(8,128)(2,1)}, bf16[512,256]{1,0:T(8,128)(2,1)S(1)}, u32[]{:S(2)}, u32[]{:S(2)}) collective-permute-start(bf16[512,256]{1,0:T(8,128)(2,1)} %wc_own), channel_id=1, source_target_pairs={{0,1},{1,0},{2,3},{3,2},{4,5},{5,4},{6,7},{7,6},{8,9},{9,8},{10,11... | collective-permute-start | bytes 786440 | tf_op jit(solution)/shard_map/ppermute | solution.py:373
  17.2 0.8 %copy-start.2 = (bf16[128,256]{1,0:T(8,128)(2,1)S(1)}, bf16[128,256]{1,0:T(8,128)(2,1)}, u32[]{:S(2)}) copy-start(bf16[128,256]{1,0:T(8,128)(2,1)} %we_own.2) | copy-start | bytes 196612
  17.2 2.1 %copy-start.3 = (bf16[256,128]{1,0:T(8,128)(2,1)S(1)}, bf16[256,128]{1,0:T(8,128)(2,1)}, u32[]{:S(2)}) copy-start(bf16[256,128]{1,0:T(8,128)(2,1)} %wd_own) | copy-start | bytes 196612
  17.3 3.6 %copy-start.1 = (bf16[512,256]{1,0:T(8,128)(2,1)S(1)}, bf16[512,256]{1,0:T(8,128)(2,1)}, u32[]{:S(2)}) copy-start(bf16[512,256]{1,0:T(8,128)(2,1)} %wc_own) | copy-start | bytes 786436
  17.3 3.6 %collective-permute-start.4 = (bf16[864,128]{1,0:T(8,128)(2,1)S(1)}, bf16[864,128]{1,0:T(8,128)(2,1)S(1)}, u32[]{:S(2)}, u32[]{:S(2)}) collective-permute-start(bf16[864,128]{1,0:T(8,128)(2,1)S(1)} %constant_dynamic-update-slice_fusion.rest), channel_id=1, source_target_pairs={{0,1},{1,0},{2,3},{3,2},{4,5},{5,4},{6,7},{7,6},{8,9},{9,8},{10,11... | collective-permute-start | bytes 663560 | tf_op jit(solution)/shard_map/ppermute | solution.py:398
  18.1 1.3 %collective-permute-start.6 = (bf16[128,256]{1,0:T(8,128)(2,1)S(1)}, bf16[128,256]{1,0:T(8,128)(2,1)S(1)}, u32[]{:S(2)}, u32[]{:S(2)}) collective-permute-start(bf16[128,256]{1,0:T(8,128)(2,1)S(1)} %copy-done.2), channel_id=1, source_target_pairs={{0,1},{1,0},{2,3},{3,2},{4,5},{5,4},{6,7},{7,6},{8,9},{9,8},{10,11... | collective-permute-start | bytes 196616 | tf_op jit(solution)/shard_map/ppermute | solution.py:373
  18.1 2.2 %collective-permute-start.5 = (bf16[288,128]{1,0:T(8,128)(2,1)S(1)}, bf16[288,128]{1,0:T(8,128)(2,1)S(1)}, u32[]{:S(2)}, u32[]{:S(2)}) collective-permute-start(bf16[288,128]{1,0:T(8,128)(2,1)S(1)} %pad_maximum_fusion.near), channel_id=1, source_target_pairs={{0,1},{1,0},{2,3},{3,2},{4,5},{5,4},{6,7},{7,6},{8,9},{9,8},{10,11... | collective-permute-start | bytes 221192 | tf_op jit(solution)/shard_map/ppermute | solution.py:372
  19.3 1.5 %collective-permute-start.9 = (bf16[256,128]{1,0:T(8,128)(2,1)S(1)}, bf16[256,128]{1,0:T(8,128)(2,1)S(1)}, u32[]{:S(2)}, u32[]{:S(2)}) collective-permute-start(bf16[256,128]{1,0:T(8,128)(2,1)S(1)} %copy-done.3), channel_id=1, source_target_pairs={{0,1},{1,0},{2,3},{3,2},{4,5},{5,4},{6,7},{7,6},{8,9},{9,8},{10,11... | collective-permute-start | bytes 196616 | tf_op jit(solution)/shard_map/ppermute | solution.py:373

commit v4 on v3

--- a/solution.py
+++ b/solution.py
@@ -12,6 +12,7 @@
 MB = 8
 CPD = 2
 ID_ROWS = 16
+EARLY = 3
 GRANT = 20 << 20
 REPLICATE_LIMIT = 1 << 20
 
@@ -77,6 +78,7 @@
     far,
     we_own,
     we_oth,
+    wd_own,
     node_part,
     cot_part,
     dec_part,
@@ -84,8 +86,9 @@
     slope,
     hit_t,
     cells,
+    gm,
+    hit,
     cots,
-    hit,
     hid,
 ):
     nodes = groups * MA * MB
@@ -112,28 +115,31 @@
     node_part[...] = mm(hit[...], hid[...])
     cot_part[...] = mm(hit[...], cot)
     dec_part[...] = mm(hid[:, :width], cot, TN)
+    gm[...] = mm(cot, wd_own[...], NT)
 
 
 def index_kernel(
-    mesh_count, tile_count, degree, near, rest, hit, reach_out, member_out, ids
+    shifts, tile_count, degree, near, rest, hit, hit_t, reach_out, member_out, ids
 ):
+    mesh_count = len(shifts)
     groups = mesh_count * tile_count
     local = MA * MB
     nodes = groups * local
-    block = near.shape[0] // tile_count
+    block = (near.shape[0] + rest.shape[0]) // groups
+    count = near.shape[0] // block
     rows = block - ID_ROWS
     my_mesh = lax.axis_index("mesh")
     my_tile = lax.axis_index("tile")
     for p in range(groups):
-        shift, turn = p // tile_count, p % tile_count
+        shift, turn = shifts[p // tile_count], p % tile_count
         group = lax.rem(my_mesh - shift + mesh_count, mesh_count) * tile_count + lax.rem(
             my_tile - turn + tile_count, tile_count
         )
-        q = p - tile_count
+        q = p - count
         tags, tags_t = tags_at(near, p * block + rows) if q < 0 else tags_at(rest, q * block + rows)
         if q >= 0:
             span = slice(q * rows, (q + 1) * rows)
-            hit[:, span] = hits(tags, tags_t, nodes)[0]
+            hit[:, span], hit_t[span, :] = hits(tags, tags_t, nodes)
         ids[pl.ds(pl.multiple_of(group * local, local), local), :] = tags_t[0:local, :]
 
     tags = ids[...].astype(jnp.int32)
@@ -168,8 +174,9 @@
     slope_near,
     hit_t_near,
     cells_near,
-    cots_near,
+    gm_near,
     hit,
+    hit_t,
     reach_ref,
     member_ref,
     we_own,
@@ -191,7 +198,7 @@
     slope,
     gpe,
     gpe_near,
-    hit_t,
+    gm,
     prediction,
     encode_grad,
     process_grad,
@@ -205,19 +212,28 @@
     core = lax.axis_index("feat")
     own = pl.ds(pl.multiple_of(core * width, width), width)
     oth = pl.ds(pl.multiple_of((1 - core) * width, width), width)
-    sent = [
-        pltpu.make_async_copy(source, target, sems.at[i])
-        for i, (source, target) in enumerate(
-            (
-                (prediction, prediction_out),
-                (encode_grad, encode_out),
-                (process_grad, process_out),
-                (coarse_grad, coarse_out),
-                (decode_grad, decode_out),
-            )
-        )
-    ]
-    nodes = hit.shape[0]
+    pairs = (
+        (prediction, prediction_out),
+        (encode_grad, encode_out),
+        (process_grad, process_out),
+        (coarse_grad, coarse_out),
+        (decode_grad, decode_out),
+    )
+
+    def half_copy(i, half):
+        source, target = pairs[i]
+        size = source.shape[0] // 2
+        part = pl.ds(pl.multiple_of(half * size, size), size)
+        return pltpu.make_async_copy(source.at[part], target.at[part], sems.at[i, half])
+
+    def launch(*chosen):
+        def start(half, carry):
+            for i in chosen:
+                half_copy(i, half).start()
+            return carry
+
+        lax.fori_loop(0, 2, start, 0)
+
     for p in range(count):
         here = pl.ds(p * block, rows)
         span = slice(p * rows, (p + 1) * rows)
@@ -232,7 +248,6 @@
         slope[span, :] = sig + act * (1.0 - sig)
         pre = mm(cell, we_oth[...])
         hid[span, width:] = (pre * jax.nn.sigmoid(pre)).astype(BF16)
-        hit_t[span, :] = hits(*tags_at(rest, p * block + rows), nodes)[1]
 
     reach = reach_ref[...]
     member = member_ref[...]
@@ -270,6 +285,7 @@
     prediction[...] = mm(merged[0], wd_own[...]) + mm(merged[1], wd_oth[...])
 
     cot = cots[...]
+    gm[...] = mm(cot, wd_own[...], NT)
     node_cot = cot_part[...] + mm(hit[...], cot)
     cot_high, cot_low = split(node_cot)
     decode_grad[...] = (
@@ -284,10 +300,6 @@
     coarse_grad[own, :] = mm(coarse_in[0], gpc[0], TN)
     coarse_grad[oth, :] = mm(coarse_in[1], gpc[0], TN)
 
-    @pl.when(core >= 0)
-    def _():
-        for i in (0, 3, 4):
-            sent[i].start()
 
     grad_coarse_in = (
         mm(gpc[0], wc_own[own, :], NT) + mm(gpc[1], wc_oth[own, :], NT),
@@ -300,24 +312,23 @@
     process_grad[own, :] = mm(agg_own, gpm[0], TN)
     process_grad[oth, :] = mm(agg_oth, gpm[0], TN)
 
-    @pl.when(core >= 0)
-    def _():
-        sent[2].start()
+    launch(0, 2, 3, 4)
 
     grad_agg = (mm(gpm[0], wp_own[own, :], NT) + mm(gpm[1], wp_oth[own, :], NT)).astype(BF16)
     grad_zero = (grad_one[0] + mm(reach, grad_agg, TN)).astype(BF16)
     for p in range(count):
         span = slice(p * rows, (p + 1) * rows)
-        grad_hidden = mm(cots[span, :], wd_own[...], NT) + mm(hit_t[span, :], grad_zero)
+        grad_hidden = gm[span, :] + mm(hit_t[span, :], grad_zero)
         gpe[span, :] = (grad_hidden * slope[span, :]).astype(BF16)
     for p in range(near_count):
         span = slice(p * rows, (p + 1) * rows)
-        grad_hidden = mm(cots_near[span, :], wd_own[...], NT) + mm(hit_t_near[span, :], grad_zero)
+        grad_hidden = gm_near[span, :] + mm(hit_t_near[span, :], grad_zero)
         gpe_near[span, :] = (grad_hidden * slope_near[span, :]).astype(BF16)
     encode_grad[...] = mm(cells[...], gpe[...], TN) + mm(cells_near[...], gpe_near[...], TN)
-    sent[1].start()
-    for copy in sent:
-        copy.wait()
+    launch(1)
+    for i in range(len(pairs)):
+        for half in range(2):
+            half_copy(i, half).wait()
 
 
 def replicated(
@@ -365,17 +376,21 @@
         columns.append(lax.ppermute(payload, "tile", ring))
     near = jnp.concatenate(columns, axis=0)
     near, weights = lax.optimization_barrier((near, weights))
-    blocks = []
-    for shift in range(1, mesh_count):
+    shifts = [0, EARLY, *[i for i in range(1, mesh_count) if i != EARLY]]
+    blocks = [near]
+    for shift in shifts[1:]:
         ring = [(i, (i + shift) % mesh_count) for i in range(mesh_count)]
         blocks.append(lax.ppermute(near, "mesh", ring))
     near_far = lax.ppermute(near, "feat", swap)
     others = tuple(lax.ppermute(w, "feat", swap) for w in weights)
+    early_far = lax.ppermute(blocks[1], "feat", swap)
+    near = jnp.concatenate(blocks[:2], axis=0)
+    near_far = jnp.concatenate([near_far, early_far], axis=0)
     degree = stencil_codes.shape[1]
-    beside = tile_count * rows
+    beside = 2 * tile_count * rows
     near_call = pl.pallas_call(
         functools.partial(near_kernel, groups),
-        in_specs=[vmem] * 4,
+        in_specs=[vmem] * 5,
         compiler_params=grant,
         out_specs=[vmem] * 8,
         out_shape=(
@@ -386,24 +401,26 @@
             pltpu.VMEM((beside, width), F32),
             pltpu.VMEM((beside, nodes), BF16),
             pltpu.VMEM((beside, c_in), BF16),
-            pltpu.VMEM((beside, c_out), BF16),
+            pltpu.VMEM((beside, width), F32),
         ),
         scratch_shapes=[
             pltpu.VMEM((nodes, beside), BF16),
+            pltpu.VMEM((beside, c_out), BF16),
             pltpu.VMEM((beside, 2 * width), BF16),
         ],
     )
-    parts = near_call(*map(held, (near, near_far, encode_weight, others[0])))
-    rest = jnp.concatenate(blocks, axis=0)
+    parts = near_call(*map(held, (near, near_far, encode_weight, others[0], decode_weight)))
+    rest = jnp.concatenate(blocks[2:], axis=0)
     rest_far = lax.ppermute(rest, "feat", swap)
-    cells = (groups - tile_count) * rows
+    cells = (groups - 2 * tile_count) * rows
     tables = pl.pallas_call(
-        functools.partial(index_kernel, mesh_count, tile_count, degree),
+        functools.partial(index_kernel, shifts, tile_count, degree),
         in_specs=[vmem] * 2,
         compiler_params=grant,
-        out_specs=[vmem] * 3,
+        out_specs=[vmem] * 4,
         out_shape=(
             pltpu.VMEM((nodes, cells), BF16),
+            pltpu.VMEM((cells, nodes), BF16),
             pltpu.VMEM((nodes, nodes), BF16),
             pltpu.VMEM((nodes, CPD * groups), BF16),
         ),
@@ -418,7 +435,7 @@
     )
     operands = [held(v) for v in (rest, rest_far, *parts, *tables, *weights, *others)]
     return pl.pallas_call(
-        functools.partial(step_kernel, tile_count),
+        functools.partial(step_kernel, 2 * tile_count),
         in_specs=[vmem] * len(operands),
         compiler_params=grant,
         out_specs=[hbm] * 5,
@@ -430,9 +447,9 @@
             pltpu.VMEM((cells, width), F32),
             pltpu.VMEM((cells, width), BF16),
             pltpu.VMEM((beside, width), BF16),
-            pltpu.VMEM((cells, nodes), BF16),
+            pltpu.VMEM((cells, width), F32),
             *[pltpu.VMEM(o.shape, F32) for o in outs],
-            pltpu.SemaphoreType.DMA((5,)),
+            pltpu.SemaphoreType.DMA((5, 2)),
         ],
     )(*operands)
 
@@ -637,7 +654,7 @@
     cells, nodes = groups * rows, groups * MA * MB
     degree = stencil_codes.shape[1]
     fits = (
-        groups > lax.axis_size("tile")
+        lax.axis_size("mesh") > 2
         and cells * nodes <= REPLICATE_LIMIT
         and lax.axis_size("feat") == 2
         and rows == c_in == rest[-1].shape[1]

time: 26.3 us -> 27.4 us (1.042)
  waiting for transfers between devices: 7.65 us -> 9.41 us
  local copies, waits for them, and re-layouts: 0.75 us -> 0.06 us
    ppermute x3, waiting for transfers between devices: 4.96 us -> 6.74 us  [replicated(): blocks.append(lax.ppermute(near, 'mesh', ring))]
    unnamed x10, local copies, waits for them, and re-layouts: 0.74 us -> 0.03 us
    ppermute x1, starting transfers between devices: 0.51 us -> 0.01 us  [replicated(): near_far = lax.ppermute(near, 'feat', swap)]
    ppermute x0 -> x1, starting transfers between devices: none -> 0.47 us  [replicated(): early_far = lax.ppermute(blocks[1], 'feat', swap)]
  transfers between devices with their start and end apart: 10 -> 11, of which waited for: 4 -> 4; matrix products, arithmetic and copies ran while one was open for 0% -> 0% of each run, Pallas kernels for 5% -> 6%
where the time goes in v4:
time: 27.4 us; the launch traced here: 27.2 us
  waiting for transfers between devices  9.41 us (34%)
  starting transfers between devices  9.39 us (34%)
  Pallas kernels  7.6 us (28%)
  between operations  0.76 us (3%)
    ppermute x3, waiting for transfers between devices, replicated(): blocks.append(lax.ppermute(near, 'mesh', ring))  6.74 us
    ppermute x3, starting transfers between devices, replicated(): blocks.append(lax.ppermute(near, 'mesh', ring))  5.2 us
    pallas_call x1, Pallas kernels, replicated(): pl.pallas_call(functools.partial(step_kernel, 2 * tile_count), in_specs=[...  4.9 us
    ppermute x1, starting transfers between devices, replicated(): columns.append(lax.ppermute(payload, 'tile', ring))  3.03 us
    ppermute x1, waiting for transfers between devices, replicated(): columns.append(lax.ppermute(payload, 'tile', ring))  1.94 us
    pallas_call x1, Pallas kernels, replicated(): pl.pallas_call(pack_kernel, in_specs=[vmem] * 6, out_specs=vmem, out_shap...  0.98 us
    pallas_call x1, Pallas kernels, replicated(): pl.pallas_call(functools.partial(index_kernel, shifts, tile_count, degree...  0.87 us
    pallas_call x1, Pallas kernels, replicated(): near_call(*map(held, (near, near_far, encode_weight, others[0], decode_we...  0.86 us
  transfers between devices with their start and end apart: 11, of which 4 were waited for; matrix products, arithmetic and copies ran while one was open for 0% of the time, Pallas kernels for 6%

profile of v4, /device:TPU:0, one launch (start us, length us, event | category | flops | bytes accessed | tf_op | source)
XLA Modules:
  0.0 27.2 jit_solution(13907435184006693922)
XLA Ops:
  0.6 0.0 copy-start.2
  0.6 1.0 %shard_map.137 = bf16[144,128]{1,0:T(8,128)(2,1)S(1)} custom-call(bf16[128,128]{1,0:T(8,128)(2,1)} %fields.1, s32[1,128]{1,0:T(1,128)} %bitcast.5, s32[1,128]{1,0:T(1,128)} %bitcast.6, s32[8,32]{1,0:T(8,128)} %bitcast.4, s32[1,32]{1,0:T(1,128)} %bitcast.7, f32[128,128]{1,0:T(8,128)} %cotangent.1), custom_call_target="tpu_custom_call" | custom-call | tf_op jit(solution)/shard_map/pallas_call | solution.py:359
  1.6 3.0 %collective-permute-start = (bf16[144,128]{1,0:T(8,128)(2,1)S(1)}, bf16[144,128]{1,0:T(8,128)(2,1)S(1)}, u32[]{:S(2)}, u32[]{:S(2)}) collective-permute-start(bf16[144,128]{1,0:T(8,128)(2,1)S(1)} %shard_map.137), channel_id=1, source_target_pairs={{0,2},{2,0},{1,3},{3,1},{4,6},{6,4},{5,7},{7,5},{8,10},{10,8},{9,1... | collective-permute-start | bytes 110600 | tf_op jit(solution)/shard_map/ppermute | solution.py:376
  4.7 1.9 %collective-permute-done = bf16[144,128]{1,0:T(8,128)(2,1)S(1)} collective-permute-done((bf16[144,128]{1,0:T(8,128)(2,1)S(1)}, bf16[144,128]{1,0:T(8,128)(2,1)S(1)}, u32[]{:S(2)}, u32[]{:S(2)}) %collective-permute-start) | collective-permute-done | bytes 36896 | tf_op jit(solution)/shard_map/ppermute | solution.py:376
  6.6 0.0 collective-permute-start.5
  6.6 4.2 %collective-permute-start.4 = (bf16[288,128]{1,0:T(8,128)(2,1)S(1)}, bf16[288,128]{1,0:T(8,128)(2,1)S(1)}, u32[]{:S(2)}, u32[]{:S(2)}) collective-permute-start(bf16[288,128]{1,0:T(8,128)(2,1)S(1)} %pad_maximum_fusion.1), channel_id=1, source_target_pairs={{0,12},{4,0},{8,4},{12,8},{1,13},{5,1},{9,5},{13,9},{2,14},{6,2},{... | collective-permute-start | bytes 221192 | tf_op jit(solution)/shard_map/ppermute | solution.py:383
  10.8 0.0 collective-permute-start.2
  10.8 1.0 %collective-permute-start.1 = (bf16[288,128]{1,0:T(8,128)(2,1)S(1)}, bf16[288,128]{1,0:T(8,128)(2,1)S(1)}, u32[]{:S(2)}, u32[]{:S(2)}) collective-permute-start(bf16[288,128]{1,0:T(8,128)(2,1)S(1)} %pad_maximum_fusion.1), channel_id=1, source_target_pairs={{0,4},{4,8},{8,12},{12,0},{1,5},{5,9},{9,13},{13,1},{2,6},{6,10},{... | collective-permute-start | bytes 221192 | tf_op jit(solution)/shard_map/ppermute | solution.py:383
  11.8 0.0 copy-done.2
  11.8 0.0 collective-permute-start.8
  11.8 5.3 %collective-permute-done.1 = bf16[288,128]{1,0:T(8,128)(2,1)S(1)} collective-permute-done((bf16[288,128]{1,0:T(8,128)(2,1)S(1)}, bf16[288,128]{1,0:T(8,128)(2,1)S(1)}, u32[]{:S(2)}, u32[]{:S(2)}) %collective-permute-start.1) | collective-permute-done | bytes 73760 | tf_op jit(solution)/shard_map/ppermute | solution.py:383
  17.1 0.0 collective-permute-start.9
  17.1 1.5 %collective-permute-done.2 = bf16[288,128]{1,0:T(8,128)(2,1)S(1)} collective-permute-done((bf16[288,128]{1,0:T(8,128)(2,1)S(1)}, bf16[288,128]{1,0:T(8,128)(2,1)S(1)}, u32[]{:S(2)}, u32[]{:S(2)}) %collective-permute-start.2) | collective-permute-done | bytes 73760 | tf_op jit(solution)/shard_map/ppermute | solution.py:383
  18.6 0.1 collective-permute-start.3
  18.7 0.0 collective-permute-done.4
  18.7 0.5 %collective-permute-start.6 = (bf16[288,128]{1,0:T(8,128)(2,1)S(1)}, bf16[288,128]{1,0:T(8,128)(2,1)S(1)}, u32[]{:S(2)}, u32[]{:S(2)}) collective-permute-start(bf16[288,128]{1,0:T(8,128)(2,1)S(1)} %collective-permute-done.4), channel_id=1, source_target_pairs={{0,1},{1,0},{2,3},{3,2},{4,5},{5,4},{6,7},{7,6},{8,9},{9,8},{10,11... | collective-permute-start | bytes 221192 | tf_op jit(solution)/shard_map/ppermute | solution.py:386
  19.2 0.0 copy-start
  19.2 0.0 copy-start.1
  19.2 0.9 %shard_map.139 = (bf16[256,512]{1,0:T(8,128)(2,1)S(1)}, bf16[512,256]{1,0:T(8,128)(2,1)S(1)}, bf16[256,256]{1,0:T(8,128)(2,1)S(1)}, bf16[256,16]{1,0:T(8,128)(2,1)S(1)}) custom-call(bf16[576,128]{1,0:T(8,128)(2,1)S(1)} %constant_dynamic-update-slice_fusion.2.near, bf16[576,128]{1,0:T(8,128)(2,1)S(1)} %constant_dynamic-update-slice_fusion.rest), custom_call_target="tpu_custom_call" | custom-call | tf_op jit(solution)/shard_map/pallas_call | solution.py:416
  20.1 0.0 collective-permute-done.5
  20.1 0.2 collective-permute-start.7
  20.3 0.0 collective-permute-done.6
  20.3 0.4 %collective-permute-start.10 = (bf16[256,128]{1,0:T(8,128)(2,1)S(1)}, bf16[256,128]{1,0:T(8,128)(2,1)S(1)}, u32[]{:S(2)}, u32[]{:S(2)}) collective-permute-start(bf16[256,128]{1,0:T(8,128)(2,1)S(1)} %copy-done.1), channel_id=1, source_target_pairs={{0,1},{1,0},{2,3},{3,2},{4,5},{5,4},{6,7},{7,6},{8,9},{9,8},{10,11... | collective-permute-start | bytes 196616 | tf_op jit(solution)/shard_map/ppermute | solution.py:385
  20.7 0.0 copy-start.3
  20.7 0.7 %collective-permute-done.7.we_oth = bf16[128,256]{1,0:T(8,128)(2,1)S(1)} collective-permute-done((bf16[128,256]{1,0:T(8,128)(2,1)S(1)}, bf16[128,256]{1,0:T(8,128)(2,1)S(1)}, u32[]{:S(2)}, u32[]{:S(2)}) %collective-permute-start.7) | collective-permute-done | bytes 65568 | tf_op jit(solution)/shard_map/ppermute | solution.py:385
  21.4 0.9 %shard_map.138 = (f32[256,512]{1,0:T(8,128)S(1)}, f32[256,128]{1,0:T(8,128)S(1)}, f32[256,128]{1,0:T(8,128)S(1)}, bf16[128,512]{1,0:T(8,128)(2,1)S(1)}, f32[512,...) custom-call(bf16[576,128]{1,0:T(8,128)(2,1)S(1)} %constant_dynamic-update-, ...), custom_call_target="tpu_custom_call" | custom-call | tf_op jit(solution)/shard_map/pallas_call | solution.py:412
  22.3 0.0 collective-permute-done.10.wd_oth
  22.3 0.0 collective-permute-done.3.far
  22.3 0.0 collective-permute-done.8.wp_oth
  22.3 0.0 collective-permute-done.9.wc_oth
  22.3 0.0 copy-done.3
  22.3 4.9 %shard_map.140 = (f32[128,128]{1,0:T(8,128)}, f32[128,256]{1,0:T(8,128)}, f32[512,256]{1,0:T(8,128)}, f32[512,256]{1,0:T(8,128)}, f32[256,128]{1,0:T(8,128)}) custom-call(bf16[576,128]{1,0:T(8,128)(2,1)S(1)} %constant_dynamic-update-slice_fusion.rest, bf16[576,128]{1,0:T(8,128)(2,1)S(1)} %collective-permute-done.3.far, ...), custom_call_target="tpu_custom_call" | custom-call | tf_op jit(solution)/shard_map/pallas_call | solution.py:437
  (8 shorter events, 0.1 us)
Async XLA Ops:
  0.6 11.2 %copy-start.2 = (bf16[512,256]{1,0:T(8,128)(2,1)S(1)}, bf16[512,256]{1,0:T(8,128)(2,1)}, u32[]{:S(2)}) copy-start(bf16[512,256]{1,0:T(8,128)(2,1)} %wp_own) | copy-start | bytes 786436
  1.6 5.0 %collective-permute-start = (bf16[144,128]{1,0:T(8,128)(2,1)S(1)}, bf16[144,128]{1,0:T(8,128)(2,1)S(1)}, u32[]{:S(2)}, u32[]{:S(2)}) collective-permute-start(bf16[144,128]{1,0:T(8,128)(2,1)S(1)} %shard_map.137), channel_id=1, source_target_pairs={{0,2},{2,0},{1,3},{3,1},{4,6},{6,4},{5,7},{7,5},{8,10},{10,8},{9,1... | collective-permute-start | bytes 110600 | tf_op jit(solution)/shard_map/ppermute | solution.py:376
  6.6 13.5 %collective-permute-start.5 = (bf16[288,128]{1,0:T(8,128)(2,1)S(1)}, bf16[288,128]{1,0:T(8,128)(2,1)S(1)}, u32[]{:S(2)}, u32[]{:S(2)}) collective-permute-start(bf16[288,128]{1,0:T(8,128)(2,1)S(1)} %pad_maximum_fusion.1), channel_id=1, source_target_pairs={{0,1},{1,0},{2,3},{3,2},{4,5},{5,4},{6,7},{7,6},{8,9},{9,8},{10,11... | collective-permute-start | bytes 221192 | tf_op jit(solution)/shard_map/ppermute | solution.py:384
  6.6 12.1 %collective-permute-start.4 = (bf16[288,128]{1,0:T(8,128)(2,1)S(1)}, bf16[288,128]{1,0:T(8,128)(2,1)S(1)}, u32[]{:S(2)}, u32[]{:S(2)}) collective-permute-start(bf16[288,128]{1,0:T(8,128)(2,1)S(1)} %pad_maximum_fusion.1), channel_id=1, source_target_pairs={{0,12},{4,0},{8,4},{12,8},{1,13},{5,1},{9,5},{13,9},{2,14},{6,2},{... | collective-permute-start | bytes 221192 | tf_op jit(solution)/shard_map/ppermute | solution.py:383
  10.8 7.8 %collective-permute-start.2 = (bf16[288,128]{1,0:T(8,128)(2,1)S(1)}, bf16[288,128]{1,0:T(8,128)(2,1)S(1)}, u32[]{:S(2)}, u32[]{:S(2)}) collective-permute-start(bf16[288,128]{1,0:T(8,128)(2,1)S(1)} %pad_maximum_fusion.1), channel_id=1, source_target_pairs={{0,8},{4,12},{8,0},{12,4},{1,9},{5,13},{9,1},{13,5},{2,10},{6,14},... | collective-permute-start | bytes 221192 | tf_op jit(solution)/shard_map/ppermute | solution.py:383
  10.8 6.3 %collective-permute-start.1 = (bf16[288,128]{1,0:T(8,128)(2,1)S(1)}, bf16[288,128]{1,0:T(8,128)(2,1)S(1)}, u32[]{:S(2)}, u32[]{:S(2)}) collective-permute-start(bf16[288,128]{1,0:T(8,128)(2,1)S(1)} %pad_maximum_fusion.1), channel_id=1, source_target_pairs={{0,4},{4,8},{8,12},{12,0},{1,5},{5,9},{9,13},{13,1},{2,6},{6,10},{... | collective-permute-start | bytes 221192 | tf_op jit(solution)/shard_map/ppermute | solution.py:383
  11.8 10.5 %collective-permute-start.8 = (bf16[512,256]{1,0:T(8,128)(2,1)S(1)}, bf16[512,256]{1,0:T(8,128)(2,1)S(1)}, u32[]{:S(2)}, u32[]{:S(2)}) collective-permute-start(bf16[512,256]{1,0:T(8,128)(2,1)S(1)} %copy-done.2), channel_id=1, source_target_pairs={{0,1},{1,0},{2,3},{3,2},{4,5},{5,4},{6,7},{7,6},{8,9},{9,8},{10,11... | collective-permute-start | bytes 786440 | tf_op jit(solution)/shard_map/ppermute | solution.py:385
  17.1 5.2 %collective-permute-start.9 = (bf16[512,256]{1,0:T(8,128)(2,1)}, bf16[512,256]{1,0:T(8,128)(2,1)S(1)}, u32[]{:S(2)}, u32[]{:S(2)}) collective-permute-start(bf16[512,256]{1,0:T(8,128)(2,1)} %wc_own), channel_id=1, source_target_pairs={{0,1},{1,0},{2,3},{3,2},{4,5},{5,4},{6,7},{7,6},{8,9},{9,8},{10,11... | collective-permute-start | bytes 786440 | tf_op jit(solution)/shard_map/ppermute | solution.py:385
  18.6 3.7 %collective-permute-start.3 = (bf16[576,128]{1,0:T(8,128)(2,1)S(1)}, bf16[576,128]{1,0:T(8,128)(2,1)S(1)}, u32[]{:S(2)}, u32[]{:S(2)}) collective-permute-start(bf16[576,128]{1,0:T(8,128)(2,1)S(1)} %constant_dynamic-update-slice_fusion.rest), channel_id=1, source_target_pairs={{0,1},{1,0},{2,3},{3,2},{4,5},{5,4},{6,7},{7,6},{8,9},{9,8},{10,11... | collective-permute-start | bytes 442376 | tf_op jit(solution)/shard_map/ppermute | solution.py:414
  18.7 1.6 %collective-permute-start.6 = (bf16[288,128]{1,0:T(8,128)(2,1)S(1)}, bf16[288,128]{1,0:T(8,128)(2,1)S(1)}, u32[]{:S(2)}, u32[]{:S(2)}) collective-permute-start(bf16[288,128]{1,0:T(8,128)(2,1)S(1)} %collective-permute-done.4), channel_id=1, source_target_pairs={{0,1},{1,0},{2,3},{3,2},{4,5},{5,4},{6,7},{7,6},{8,9},{9,8},{10,11... | collective-permute-start | bytes 221192 | tf_op jit(solution)/shard_map/ppermute | solution.py:386
  19.2 0.9 %copy-start = (bf16[128,256]{1,0:T(8,128)(2,1)S(1)}, bf16[128,256]{1,0:T(8,128)(2,1)}, u32[]{:S(2)}) copy-start(bf16[128,256]{1,0:T(8,128)(2,1)} %we_own.2) | copy-start | bytes 196612
  19.2 1.1 %copy-start.1 = (bf16[256,128]{1,0:T(8,128)(2,1)S(1)}, bf16[256,128]{1,0:T(8,128)(2,1)}, u32[]{:S(2)}) copy-start(bf16[256,128]{1,0:T(8,128)(2,1)} %wd_own.2) | copy-start | bytes 196612
  20.1 1.3 %collective-permute-start.7 = (bf16[128,256]{1,0:T(8,128)(2,1)S(1)}, bf16[128,256]{1,0:T(8,128)(2,1)S(1)}, u32[]{:S(2)}, u32[]{:S(2)}) collective-permute-start(bf16[128,256]{1,0:T(8,128)(2,1)S(1)} %copy-done), channel_id=1, source_target_pairs={{0,1},{1,0},{2,3},{3,2},{4,5},{5,4},{6,7},{7,6},{8,9},{9,8},{10,11... | collective-permute-start | bytes 196616 | tf_op jit(solution)/shard_map/ppermute | solution.py:385
  20.3 2.0 %collective-permute-start.10 = (bf16[256,128]{1,0:T(8,128)(2,1)S(1)}, bf16[256,128]{1,0:T(8,128)(2,1)S(1)}, u32[]{:S(2)}, u32[]{:S(2)}) collective-permute-start(bf16[256,128]{1,0:T(8,128)(2,1)S(1)} %copy-done.1), channel_id=1, source_target_pairs={{0,1},{1,0},{2,3},{3,2},{4,5},{5,4},{6,7},{7,6},{8,9},{9,8},{10,11... | collective-permute-start | bytes 196616 | tf_op jit(solution)/shard_map/ppermute | solution.py:385
  20.7 1.6 %copy-start.3 = (bf16[512,256]{1,0:T(8,128)(2,1)S(1)}, bf16[512,256]{1,0:T(8,128)(2,1)}, u32[]{:S(2)}) copy-start(bf16[512,256]{1,0:T(8,128)(2,1)} %wc_own) | copy-start | bytes 786436
